TPU v7x, 8 devices: a whole 2x2x1 slice. The times are simulated.
8 devices in a mesh: col: 4 (over z, y, x), row: 2 (over core).
Axes of the slice: x: 2, y: 2, z: 1, core: 2. Of those that a mesh axis runs over, the one named last changes fastest.
Arguments:
- features: bfloat16 [131072, 128], P(('row', 'col'))
- w_hidden: bfloat16 [128, 256], replicated
- w_output: bfloat16 [256, 40], replicated
- adj_cols: int32 [16, 131072], P('col', 'row')
- adj_vals: bfloat16 [16, 131072], P('col', 'row')
- adj_mask: int32 [16, 131072], P('col', 'row')
- labels: int32 [131072], P(('row', 'col'))
- train_mask: int32 [131072], P(('row', 'col'))
Outputs:
- output 1: float32 [], replicated
- output 2: float32 [128, 256], replicated
- output 3: float32 [256, 40], replicated
All inputs are finite; a program needn't handle non-finite values.
Results may differ from a plain program's by a relative error of at most 0.001.
Values are sent between devices in bfloat16 or wider.
A program may use at most 1 GiB of HBM per device.

v0:
```python
import jax
import jax.numpy as jnp
from jax import lax
from jax.sharding import PartitionSpec as P

CONTRACT_ROWS = (((0,), (0,)), ((), ()))
CONTRACT_COLS = (((1,), (1,)), ((), ()))


def gather_apply(col_ids_all, weights, dense):
    def slot_step(running, slot):
        col_ids, slot_w = slot
        return running + slot_w[:, None] * jnp.take(dense, col_ids, axis=0), None
    zero_acc = jnp.zeros((col_ids_all.shape[1], dense.shape[1]), jnp.float32)
    summed, _ = lax.scan(slot_step, zero_acc, (col_ids_all, weights))
    return summed


def scatter_apply(col_ids_all, weights, dense, num_out):
    def slot_step(running, slot):
        col_ids, slot_w = slot
        return running + jax.ops.segment_sum(slot_w[:, None] * dense, col_ids, num_segments=num_out), None
    zero_acc = jnp.zeros((num_out, dense.shape[1]), jnp.float32)
    summed, _ = lax.scan(slot_step, zero_acc, (col_ids_all, weights))
    return summed


def solution(mesh):
    row_size = mesh.shape["row"]
    col_size = mesh.shape["col"]
    both_axes = ("col", "row")
    to_source = [(col_j * row_size + row_i, row_i * col_size + col_j) for row_i in range(row_size) for col_j in range(col_size)]
    to_dest = [(flat_idx, (flat_idx % col_size) * row_size + flat_idx // col_size) for flat_idx in range(row_size * col_size)]

    def device_step(feat_blk, w_hidden, w_output, cols_blk, vals_blk, mask_blk, labels_blk, train_blk):
        col_nodes = feat_blk.shape[0] * row_size
        weights = vals_blk.astype(jnp.float32) * mask_blk.astype(jnp.float32)
        feat_src = lax.ppermute(feat_blk, both_axes, to_source)
        proj_one = jnp.dot(feat_src, w_hidden, preferred_element_type=jnp.float32).astype(jnp.bfloat16)
        dense_one = lax.all_gather(proj_one, "row", axis=0, tiled=True)
        part_one = gather_apply(cols_blk, weights, dense_one)
        z_one = lax.psum_scatter(part_one, "col", scatter_dimension=0, tiled=True).astype(jnp.bfloat16)
        h_one = jnp.maximum(z_one, 0)
        proj_two = jnp.dot(h_one, w_output, preferred_element_type=jnp.float32).astype(jnp.bfloat16)
        proj_src = lax.ppermute(proj_two, both_axes, to_source)
        dense_two = lax.all_gather(proj_src, "row", axis=0, tiled=True)
        part_two = gather_apply(cols_blk, weights, dense_two)
        z_two = lax.psum_scatter(part_two, "col", scatter_dimension=0, tiled=True)
        mask_f = train_blk.astype(jnp.float32)
        train_count = jnp.maximum(lax.psum(jnp.sum(train_blk), both_axes), 1).astype(jnp.float32)
        log_norm = jax.nn.logsumexp(z_two, axis=1)
        onehot = (labels_blk[:, None] == jnp.arange(z_two.shape[1], dtype=jnp.int32)[None, :]).astype(jnp.float32)
        picked = jnp.sum(z_two * onehot, axis=1)
        loss_mean = lax.psum(jnp.sum(mask_f * (log_norm - picked)), both_axes) / train_count
        softmax_z = jnp.exp(z_two - log_norm[:, None])
        grad_two = ((mask_f / train_count)[:, None] * (softmax_z - onehot)).astype(jnp.bfloat16)
        grad_rows = lax.all_gather(grad_two, "col", axis=0, tiled=True)
        part_back = scatter_apply(cols_blk, weights, grad_rows, col_nodes)
        back_src = lax.psum_scatter(part_back, "row", scatter_dimension=0, tiled=True).astype(jnp.bfloat16)
        back_two = lax.ppermute(back_src, both_axes, to_dest)
        grad_w_output = lax.dot_general(h_one, back_two, CONTRACT_ROWS, preferred_element_type=jnp.float32)
        dh_one = lax.dot_general(back_two, w_output, CONTRACT_COLS, preferred_element_type=jnp.float32)
        dz_one = jnp.where(z_one > 0, dh_one, 0.0).astype(jnp.bfloat16)
        dz_rows = lax.all_gather(dz_one, "col", axis=0, tiled=True)
        part_dz = scatter_apply(cols_blk, weights, dz_rows, col_nodes)
        back_one = lax.psum_scatter(part_dz, "row", scatter_dimension=0, tiled=True).astype(jnp.bfloat16)
        grad_w_hidden = lax.dot_general(feat_src, back_one, CONTRACT_ROWS, preferred_element_type=jnp.float32)
        grad_w_hidden = lax.psum(grad_w_hidden, both_axes)
        grad_w_output = lax.psum(grad_w_output, both_axes)
        return loss_mean, grad_w_hidden, grad_w_output

    node_spec = P(("row", "col"), None)
    label_spec = P(("row", "col"))
    adj_spec = P("col", "row")
    return jax.shard_map(device_step, mesh=mesh, in_specs=(node_spec, P(), P(), adj_spec, adj_spec, adj_spec, label_spec, label_spec), out_specs=(P(), P(), P()), check_vma=False)
```

profile of v0, /device:TPU:0, one launch (start us, length us, event | category | flops | bytes accessed | tf_op | source)
XLA Modules:
  0.0 7098.8 jit_solution(6502407720060989294)
XLA Ops:
  7.2 3.0 collective-permute-start
  10.2 2.0 copy-done.3
  12.2 5.5 convolution_convert_fusion
  17.8 1.3 convert_multiply_fusion
  19.2 121.3 %all-gather.5.cloned.1.call-done = bf16[32768,256]{1,0:T(8,128)(2,1)} async-done(((bf16[16384,256]{1,0:T(8,128)(2,1)}), bf16[32768,256]{1,0:T(8,128)(2,1)}) %all-gather.5.cloned.1.call-update) | async-done | bytes 16777232 | tf_op jit(solution)/shard_map/all_gather | solution.py:40
  140.5 1212.5 %while.44 = (s32[]{:T(128)}, f32[65536,256]{1,0:T(8,128)}, f32[4,65536]{1,0:T(4,128)S(1)}, s32[4,65536]{1,0:T(4,128)S(1)}, bf16[32768,256]{1,0:T(8,128)(2,1)}, /*index=5*/s32[]{:T(128)}, s32[]{:T(128)}) while((s32[]{:T(128)}, f32[65536,256]{1,0:T(8,128)}, f32[4,65536]{1,0:T(4,128)S(1)}, s32[4,65536]{1,0:T(4,128)S(1)}, ...), condition=%wide.region_1.2_spmd.clone, body=%wide.region_0.1_spmd.clone.sunk | while | flops 84541440 | bytes 237633648 | solution.py:15
  141.0 250.0 %gather_fusion = bf16[65536,256]{1,0:T(8,128)(2,1)} fusion(bf16[32768,256]{1,0:T(8,128)(2,1)} %get-tuple-element.376, s32[65536]{0:T(1024)S(1)} %broadcast_clamp_fusion.4), kind=kCustom, calls=%fused_computation.clone.clone.1 | custom fusion | bytes 67371008 | tf_op jit(solution)/shard_map/while/body/eval_jaxpr/jit(_take)/gather | solution.py:13
  391.3 50.6 select_add_fusion.4
  441.9 0.4 compare_select_fusion.6
  442.3 250.0 %gather_fusion = bf16[65536,256]{1,0:T(8,128)(2,1)} fusion(bf16[32768,256]{1,0:T(8,128)(2,1)} %get-tuple-element.376, s32[65536]{0:T(1024)S(1)} %broadcast_clamp_fusion.4), kind=kCustom, calls=%fused_computation.clone.clone.1 | custom fusion | bytes 67371008 | tf_op jit(solution)/shard_map/while/body/eval_jaxpr/jit(_take)/gather | solution.py:13
  692.6 52.9 select_add_fusion.4
  746.1 250.0 %gather_fusion = bf16[65536,256]{1,0:T(8,128)(2,1)} fusion(bf16[32768,256]{1,0:T(8,128)(2,1)} %get-tuple-element.376, s32[65536]{0:T(1024)S(1)} %broadcast_clamp_fusion.4), kind=kCustom, calls=%fused_computation.clone.clone.1 | custom fusion | bytes 67371008 | tf_op jit(solution)/shard_map/while/body/eval_jaxpr/jit(_take)/gather | solution.py:13
  996.4 52.9 select_add_fusion.4
  1049.3 0.4 compare_select_fusion.6
  1049.8 250.0 %gather_fusion = bf16[65536,256]{1,0:T(8,128)(2,1)} fusion(bf16[32768,256]{1,0:T(8,128)(2,1)} %get-tuple-element.376, s32[65536]{0:T(1024)S(1)} %broadcast_clamp_fusion.4), kind=kCustom, calls=%fused_computation.clone.clone.1 | custom fusion | bytes 67371008 | tf_op jit(solution)/shard_map/while/body/eval_jaxpr/jit(_take)/gather | solution.py:13
  1300.1 52.9 select_add_fusion.4
  1353.1 553.7 %reduce-scatter.13.cloned.1.call-done = f32[16384,256]{1,0:T(8,128)} async-done(((f32[65536,256]{1,0:T(8,128)}), f32[16384,256]{1,0:T(8,128)}) %reduce-scatter.13.cloned.1.call-update) | async-done | bytes 16777232
  1906.8 8.4 convolution_convert_fusion.1
  1915.2 1.7 collective-permute-start.1
  1917.2 39.8 all-gather.7.cloned.1.call-done
  1957.0 7.9 copy.15
  1965.0 1007.7 %while.45 = (s32[]{:T(128)}, f32[65536,40]{1,0:T(8,128)}, f32[4,65536]{1,0:T(4,128)S(1)}, s32[4,65536]{1,0:T(4,128)S(1)}, bf16[32768,40]{1,0:T(8,128)(2,1)}, /*index=5*/s32[]{:T(128)}, s32[]{:T(128)}) while((s32[]{:T(128)}, f32[65536,40]{1,0:T(8,128)}, f32[4,65536]{1,0:T(4,128)S(1)}, s32[4,65536]{1,0:T(4,128)S(1)}, ...), condition=%wide.region_4.5_spmd.clone, body=%wide.region_3.4_spmd.clone.sunk | while | flops 13762563 | bytes 39452764 | solution.py:15
  1965.5 223.8 %gather_fusion.1 = bf16[65536,40]{1,0:T(8,128)(2,1)} fusion(bf16[32768,40]{1,0:T(8,128)(2,1)} %get-tuple-element.397, s32[65536]{0:T(1024)S(1)} %broadcast_clamp_fusion.5), kind=kCustom, calls=%fused_computation.1.clone.clone.1 | custom fusion | bytes 10747904 | tf_op jit(solution)/shard_map/while/body/eval_jaxpr/jit(_take)/gather | solution.py:13
  2189.6 25.5 select_add_fusion.5
  2215.6 223.9 %gather_fusion.1 = bf16[65536,40]{1,0:T(8,128)(2,1)} fusion(bf16[32768,40]{1,0:T(8,128)(2,1)} %get-tuple-element.397, s32[65536]{0:T(1024)S(1)} %broadcast_clamp_fusion.5), kind=kCustom, calls=%fused_computation.1.clone.clone.1 | custom fusion | bytes 10747904 | tf_op jit(solution)/shard_map/while/body/eval_jaxpr/jit(_take)/gather | solution.py:13
  2439.7 27.9 select_add_fusion.5
  2468.1 223.8 %gather_fusion.1 = bf16[65536,40]{1,0:T(8,128)(2,1)} fusion(bf16[32768,40]{1,0:T(8,128)(2,1)} %get-tuple-element.397, s32[65536]{0:T(1024)S(1)} %broadcast_clamp_fusion.5), kind=kCustom, calls=%fused_computation.1.clone.clone.1 | custom fusion | bytes 10747904 | tf_op jit(solution)/shard_map/while/body/eval_jaxpr/jit(_take)/gather | solution.py:13
  2692.3 27.9 select_add_fusion.5
  2720.7 223.8 %gather_fusion.1 = bf16[65536,40]{1,0:T(8,128)(2,1)} fusion(bf16[32768,40]{1,0:T(8,128)(2,1)} %get-tuple-element.397, s32[65536]{0:T(1024)S(1)} %broadcast_clamp_fusion.5), kind=kCustom, calls=%fused_computation.1.clone.clone.1 | custom fusion | bytes 10747904 | tf_op jit(solution)/shard_map/while/body/eval_jaxpr/jit(_take)/gather | solution.py:13
  2944.8 27.9 select_add_fusion.5
  2972.8 0.7 copy-done.8
  2973.6 0.6 reduce_sum.39
  2974.2 24.3 psum.29
  2999.1 259.0 %reduce-scatter.7.cloned.1.call-done = f32[16384,40]{1,0:T(8,128)} async-done(((f32[65536,40]{1,0:T(8,128)}), f32[16384,40]{1,0:T(8,128)}) %reduce-scatter.7.cloned.1.call-update) | async-done | bytes 2621456 | tf_op jit(solution)/shard_map/reduce_scatter | solution.py:48
  3258.1 4.6 reduce_max.9
  3262.8 11.4 select_reduce_fusion
  3274.2 0.7 multiply_reduce_fusion
  3274.9 13.9 multiply_convert_fusion
  3288.9 151.9 %all-gather.9.cloned.1.call-done = bf16[65536,40]{1,0:T(8,128)(2,1)} async-done(((bf16[16384,40]{1,0:T(8,128)(2,1)}), bf16[65536,40]{1,0:T(8,128)(2,1)}) %all-gather.9.cloned.1.call-update) | async-done | bytes 5242896 | tf_op jit(solution)/shard_map/all_gather | solution.py:57
  3440.8 6.0 broadcast.74
  3446.8 1570.8 %while.42 = (s32[]{:T(128)}, f32[32768,40]{1,0:T(8,128)}, s32[4,65536]{1,0:T(4,128)S(1)}, f32[4,65536]{1,0:T(4,128)S(1)}, bf16[65536,40]{1,0:T(8,128)(2,1)}, /*index=5*/s32[]{:T(128)}) while((s32[]{:T(128)}, f32[32768,40]{1,0:T(8,128)}, s32[4,65536]{1,0:T(4,128)S(1)}, f32[4,65536]{1,0:T(4,128)S(1)}, bf16[65536,40]{1,0:T(8,128)(2,1)}, ...), condition=%wide.region_15.16_spmd, body=%wide.region_13.15_spmd.sunk | while | flops 7864322 | bytes 23330892 | solution.py:24
  3447.3 392.2 %scatter_custom_fusion.9 = f32[32768,40]{1,0:T(8,128)} fusion(f32[32768,40]{1,0:T(8,128)} %get-tuple-element.407, s32[65536]{0:T(1024)S(1)} %bitcast.56, bf16[65536,40]{1,0:T(8,128)(2,1)} %get-tuple-element.416, f32[65536]{0:T(1024)S(1)} %bitcast.50), kind=kCustom, calls=%fused_computation.4.clone.1 | custom fusion | flops 7864320 | bytes 22282240 | tf_op jit(solution)/shard_map/while/body/eval_jaxpr/scatter-add | solution.py:22
  3840.0 392.2 %scatter_custom_fusion.9 = f32[32768,40]{1,0:T(8,128)} fusion(f32[32768,40]{1,0:T(8,128)} %get-tuple-element.407, s32[65536]{0:T(1024)S(1)} %bitcast.56, bf16[65536,40]{1,0:T(8,128)(2,1)} %get-tuple-element.416, f32[65536]{0:T(1024)S(1)} %bitcast.50), kind=kCustom, calls=%fused_computation.4.clone.1 | custom fusion | flops 7864320 | bytes 22282240 | tf_op jit(solution)/shard_map/while/body/eval_jaxpr/scatter-add | solution.py:22
  4232.7 392.2 %scatter_custom_fusion.9 = f32[32768,40]{1,0:T(8,128)} fusion(f32[32768,40]{1,0:T(8,128)} %get-tuple-element.407, s32[65536]{0:T(1024)S(1)} %bitcast.56, bf16[65536,40]{1,0:T(8,128)(2,1)} %get-tuple-element.416, f32[65536]{0:T(1024)S(1)} %bitcast.50), kind=kCustom, calls=%fused_computation.4.clone.1 | custom fusion | flops 7864320 | bytes 22282240 | tf_op jit(solution)/shard_map/while/body/eval_jaxpr/scatter-add | solution.py:22
  4625.4 392.2 %scatter_custom_fusion.9 = f32[32768,40]{1,0:T(8,128)} fusion(f32[32768,40]{1,0:T(8,128)} %get-tuple-element.407, s32[65536]{0:T(1024)S(1)} %bitcast.56, bf16[65536,40]{1,0:T(8,128)(2,1)} %get-tuple-element.416, f32[65536]{0:T(1024)S(1)} %bitcast.50), kind=kCustom, calls=%fused_computation.4.clone.1 | custom fusion | flops 7864320 | bytes 22282240 | tf_op jit(solution)/shard_map/while/body/eval_jaxpr/scatter-add | solution.py:22
  5017.6 11.8 copy.16
  5029.4 9.7 reduce-scatter.9.cloned.1.call-done
  5039.1 1.9 convert_element_type.57
  5040.9 0.7 collective-permute-start.2
  5041.7 1.1 copy-done.4
  5042.8 11.4 fusion.8
  5054.5 311.3 %all-gather.11.cloned.1.call-done = bf16[65536,256]{1,0:T(8,128)(2,1)} async-done(((bf16[16384,256]{1,0:T(8,128)(2,1)}), bf16[65536,256]{1,0:T(8,128)(2,1)}) %all-gather.11.cloned.1.call-update) | async-done | bytes 33554448 | tf_op jit(solution)/shard_map/all_gather | solution.py:64
  5365.8 11.0 broadcast.73
  5376.8 1619.7 %while.43 = (s32[]{:T(128)}, f32[32768,256]{1,0:T(8,128)}, s32[4,65536]{1,0:T(4,128)S(1)}, f32[4,65536]{1,0:T(4,128)S(1)}, bf16[65536,256]{1,0:T(8,128)(2,1)}, /*index=5*/s32[]{:T(128)}) while((s32[]{:T(128)}, f32[32768,256]{1,0:T(8,128)}, s32[4,65536]{1,0:T(4,128)S(1)}, f32[4,65536]{1,0:T(4,128)S(1)}, bf16[65536,256]{1,0:T(8,128)(2,1)}, ...), condition=%wide.region_19.20_spmd, body=%wide.region_17.19_spmd.sunk | while | flops 50331648 | bytes 68419656 | solution.py:24
  5377.3 404.5 %scatter_custom_fusion.11 = f32[32768,256]{1,0:T(8,128)} fusion(f32[32768,256]{1,0:T(8,128)} %get-tuple-element.425, s32[65536]{0:T(1024)S(1)} %bitcast.57, bf16[65536,256]{1,0:T(8,128)(2,1)} %get-tuple-element.434, f32[65536]{0:T(1024)S(1)} %bitcast.51), kind=kCustom, calls=%fused_computation.10.clone.1 | custom fusion | flops 50331648 | bytes 67371008 | tf_op jit(solution)/shard_map/while/body/eval_jaxpr/scatter-add | solution.py:22
  5782.2 404.5 %scatter_custom_fusion.11 = f32[32768,256]{1,0:T(8,128)} fusion(f32[32768,256]{1,0:T(8,128)} %get-tuple-element.425, s32[65536]{0:T(1024)S(1)} %bitcast.57, bf16[65536,256]{1,0:T(8,128)(2,1)} %get-tuple-element.434, f32[65536]{0:T(1024)S(1)} %bitcast.51), kind=kCustom, calls=%fused_computation.10.clone.1 | custom fusion | flops 50331648 | bytes 67371008 | tf_op jit(solution)/shard_map/while/body/eval_jaxpr/scatter-add | solution.py:22
  6187.2 404.5 %scatter_custom_fusion.11 = f32[32768,256]{1,0:T(8,128)} fusion(f32[32768,256]{1,0:T(8,128)} %get-tuple-element.425, s32[65536]{0:T(1024)S(1)} %bitcast.57, bf16[65536,256]{1,0:T(8,128)(2,1)} %get-tuple-element.434, f32[65536]{0:T(1024)S(1)} %bitcast.51), kind=kCustom, calls=%fused_computation.10.clone.1 | custom fusion | flops 50331648 | bytes 67371008 | tf_op jit(solution)/shard_map/while/body/eval_jaxpr/scatter-add | solution.py:22
  6592.1 404.5 %scatter_custom_fusion.11 = f32[32768,256]{1,0:T(8,128)} fusion(f32[32768,256]{1,0:T(8,128)} %get-tuple-element.425, s32[65536]{0:T(1024)S(1)} %bitcast.57, bf16[65536,256]{1,0:T(8,128)(2,1)} %get-tuple-element.434, f32[65536]{0:T(1024)S(1)} %bitcast.51), kind=kCustom, calls=%fused_computation.10.clone.1 | custom fusion | flops 50331648 | bytes 67371008 | tf_op jit(solution)/shard_map/while/body/eval_jaxpr/scatter-add | solution.py:22
  6996.7 39.3 reduce-scatter.11.cloned.1.call-done
  7036.0 10.0 fusion.16
  7046.0 7.3 fusion.11
  7053.3 24.4 all-reduce.1
  7078.4 11.1 all-reduce.4.cloned.1.call-done
  7089.4 1.7 copy.17
  (89 shorter events, 10.0 us)
Async XLA Ops:
  7.2 5.0 copy-start
  7.2 10.7 copy-start.6
  7.2 133.3 %copy-start.2 = (s32[4,65536]{1,0:T(4,128)S(1)}, s32[4,65536]{1,0:T(4,128)}, u32[]{:S(2)}) copy-start(s32[4,65536]{1,0:T(4,128)} %param.19) | copy-start | bytes 3145732
  7.2 133.3 %all-gather.5.cloned.1.call-start = ((), (), s32[]{:S(2)}) async-start(), calls=%async_computation.4 | async-start | bytes 25165824 | tf_op jit(solution)/shard_map/all_gather | solution.py:40
  7.2 3.0 collective-permute-start
  10.2 2.0 copy-start.3
  17.8 1889.0 %reduce-scatter.13.cloned.1.call-start = ((), (), s32[]{:S(2)}) async-start(), calls=%async_computation.12 | async-start | bytes 83886080
  1353.0 553.8 %copy-start.9 = (bf16[256,40]{0,1:T(8,128)(2,1)S(1)}, bf16[256,40]{0,1:T(8,128)(2,1)}, u32[]{:S(2)}) copy-start(bf16[256,40]{0,1:T(8,128)(2,1)} %param.18) | copy-start | bytes 61444
  1353.1 604.0 %all-gather.7.cloned.1.call-start = ((), (), s32[]{:S(2)}) async-start(), calls=%async_computation.5 | async-start | bytes 3932160 | tf_op jit(solution)/shard_map/all_gather | solution.py:46
  1915.2 1.7 collective-permute-start.1
  1917.0 1341.2 %reduce-scatter.7.cloned.1.call-start = ((), (), s32[]{:S(2)}) async-start(), calls=%async_computation.6 | async-start | bytes 41943040 | tf_op jit(solution)/shard_map/reduce_scatter | solution.py:48
  2972.7 0.8 copy-start.8
  2972.7 290.0 %copy-start.7 = (s32[16384]{0:T(1024)S(1)}, s32[16384]{0:T(1024)}, u32[]{:S(2)}) copy-start(s32[16384]{0:T(1024)} %param.22) | copy-start | bytes 196612
  2972.8 468.0 %all-gather.9.cloned.1.call-start = ((), (), s32[]{:S(2)}) async-start(), calls=%async_computation.7 | async-start | bytes 20971520 | tf_op jit(solution)/shard_map/all_gather | solution.py:57
  3288.8 1750.3 %reduce-scatter.9.cloned.1.call-start = ((), (), s32[]{:S(2)}) async-start(), calls=%async_computation.8 | async-start | bytes 7864320 | tf_op jit(solution)/shard_map/reduce_scatter | solution.py:59
  5017.6 25.2 copy-start.10
  5029.4 336.5 %all-gather.11.cloned.1.call-start = ((), (), s32[]{:S(2)}) async-start(), calls=%async_computation.9 | async-start | bytes 41943040 | tf_op jit(solution)/shard_map/all_gather | solution.py:64
  5040.9 0.8 collective-permute-start.2
  5041.7 1.1 copy-start.4
  5054.3 1981.7 %reduce-scatter.11.cloned.1.call-start = ((), (), s32[]{:S(2)}) async-start(), calls=%async_computation.10 | async-start | bytes 50331648 | tf_op jit(solution)/shard_map/reduce_scatter | solution.py:66
  6996.6 49.4 copy-start.5
  6996.6 94.5 %copy-start.1 = (bf16[128,256]{1,0:T(8,128)(2,1)S(1)}, bf16[128,256]{1,0:T(8,128)(2,1)}, u32[]{:S(2)}) copy-start(bf16[128,256]{1,0:T(8,128)(2,1)} %param.17) | copy-start | bytes 196612
  6996.6 92.8 %all-reduce.4.cloned.1.call-start = ((), (), s32[]{:S(2)}) async-start(), calls=%async_computation.11 | async-start | bytes 262144 | tf_op jit(solution)/shard_map/psum | solution.py:68
Sparse Core Ops, SparseCore 0:
  17.9 122.5 all-gather.4
  1353.2 553.5 reduce-scatter.12
  1917.1 39.8 all-gather.6
  2972.9 285.1 reduce-scatter.6
  3288.9 151.8 all-gather.8
  5029.5 9.5 reduce-scatter.8
  5054.4 311.3 all-gather.10
  6996.7 39.1 reduce-scatter.10
  7046.1 43.2 all-reduce.3
where the time goes:
time: 7100 us
  other arithmetic  3540 us (50%)
  local copies, waits for them, and re-layouts  1940 us (27%)
  waiting for transfers between devices  1500 us (21%)
    scatter-add x8, other arithmetic, slot_step(): jax.ops.segment_sum(slot_w[:, None] * dense, col_ids, num_segments=num_out)  3190 us
    gather x8, local copies, waits for them, and re-layouts, slot_step(): return (running + slot_w[:, None] * jnp.take(dense, col_ids, axis=0), None)  1900 us
    unnamed x10, waiting for transfers between devices  554 us
    add x8, other arithmetic, slot_step(): return (running + slot_w[:, None] * jnp.take(dense, col_ids, axis=0), None)  318 us
    all_gather x1, waiting for transfers between devices, device_step(): dz_rows = lax.all_gather(dz_one, 'col', axis=0, tiled=True)  311 us
    reduce_scatter x1, waiting for transfers between devices, device_step(): z_two = lax.psum_scatter(part_two, 'col', scatter_dimension=0, tiled=True)  259 us
    all_gather x1, waiting for transfers between devices, device_step(): grad_rows = lax.all_gather(grad_two, 'col', axis=0, tiled=True)  152 us
  transfers between devices with their start and end apart: 12, of which 9 were waited for; matrix products, arithmetic and copies ran while one was open for 0% of the time, Pallas kernels for 0%

commit v1 on v0

v1 whole, which is shorter than its diff:
```python
import functools

import jax
import jax.numpy as jnp
from jax import lax
from jax.experimental import pallas as pl
from jax.experimental.pallas import tpu as pltpu
from jax.sharding import PartitionSpec as P

CONTRACT_ROWS = (((0,), (0,)), ((), ()))
CONTRACT_COLS = (((1,), (1,)), ((), ()))
LANES = 128
TILE_ROWS = 512
UNROLL = 32
CHUNK = 256
STEP_CHUNKS = 4
COL_TILE = 128
VMEM = 60 << 20


def copy_rows(idx_ref, first, count, table, stage, stage_first, width):
    def body(group, carry):
        edge = pl.multiple_of(group * UNROLL, UNROLL)
        ids = idx_ref.at[pl.ds(first + edge, UNROLL)]
        out = stage.at[pl.ds(pl.multiple_of(stage_first + width * edge, width * UNROLL), width * UNROLL)]
        for u in range(UNROLL):
            if width == 1:
                out[u, :] = table[ids[u], :]
            else:
                out[width * u:width * (u + 1), :] = table[pl.ds(pl.multiple_of(ids[u], width), width), :]
        return carry
    lax.fori_loop(0, count // UNROLL, body, 0)


def store_table(table, first, value, width):
    rows = value.shape[0]
    for part in range(width):
        piece = value[:, part * LANES:(part + 1) * LANES]
        if width == 1:
            table[pl.ds(pl.multiple_of(first, rows), rows), :] = piece
        else:
            table[pl.ds(width * first + part, rows, stride=width), :] = piece


def stream_rows(sources, buffers, sems, first_row, total, chunk, use):
    steps = total // chunk

    def copies(step, slot):
        start = pl.multiple_of(first_row + step * chunk, chunk)
        return [pltpu.make_async_copy(src.at[pl.ds(start, chunk), :], buf.at[slot], sems.at[n, slot])
                for n, (src, buf) in enumerate(zip(sources, buffers))]
    for c in copies(0, 0):
        c.start()

    def body(step, carry):
        slot = lax.rem(step, 2)
        for c in copies(step, slot):
            c.wait()

        @pl.when(step + 1 < steps)
        def _():
            for c in copies(step + 1, 1 - slot):
                c.start()
        use([buf.at[slot] for buf in buffers], step * chunk)
        return carry
    lax.fori_loop(0, steps, body, 0)


def weighted_sum(stage, w_ref, block, width):
    slots = w_ref.shape[1]
    w_rows = w_ref[0, :, block * LANES:(block + 1) * LANES]
    w_rows = jnp.concatenate([w_rows] * (8 // slots), axis=0)
    w_cols = w_rows.T
    parts = []
    for part in range(width):
        total = None
        for slot in range(slots):
            at = width * (slot * TILE_ROWS + block * LANES)
            rows = stage[pl.ds(at + part, LANES, stride=width), :] if width > 1 else stage[at:at + LANES, :]
            term = w_cols[:, slot:slot + 1] * rows
            total = term if total is None else total + term
        parts.append(total)
    return parts


def layer_one_kernel(idx_ref, w_ref, x_hbm, w_hidden, w_output, z_ref, p_ref, table, acc, stage, x_buf, sems):
    phase, tile = pl.program_id(0), pl.program_id(1)
    col_nodes = table.shape[0] // 2

    @pl.when(tile == 0)
    def _():
        def use(bufs, offset):
            for sub in range(0, x_buf.shape[1], 256):
                proj = jnp.dot(bufs[0][sub:sub + 256, :], w_hidden[...], preferred_element_type=jnp.float32)
                proj = proj.astype(jnp.bfloat16).astype(jnp.float32)
                store_table(table, offset + sub, proj, 2)
        stream_rows([x_hbm], [x_buf], sems, phase * col_nodes, col_nodes, x_buf.shape[1], use)

    copy_rows(idx_ref, 0, idx_ref.shape[0], table, stage, 0, 2)
    for block in range(TILE_ROWS // LANES):
        parts = weighted_sum(stage, w_ref, block, 2)
        rows = pl.ds(pl.multiple_of(tile * TILE_ROWS + block * LANES, LANES), LANES)

        @pl.when(phase == 0)
        def _():
            for part in range(2):
                acc[rows, part * LANES:(part + 1) * LANES] = parts[part]

        @pl.when(phase > 0)
        def _():
            for part in range(2):
                acc[rows, part * LANES:(part + 1) * LANES] += parts[part]

    @pl.when(phase == pl.num_programs(0) - 1)
    def _():
        rows = pl.ds(pl.multiple_of(tile * TILE_ROWS, TILE_ROWS), TILE_ROWS)
        z_one = acc[rows, :].astype(jnp.bfloat16)
        z_ref[...] = z_one
        h_one = jnp.maximum(z_one, 0)
        p_ref[...] = jnp.dot(h_one, w_output[...], preferred_element_type=jnp.float32).astype(jnp.bfloat16)


def layer_two_kernel(idx_ref, w_ref, p_hbm, z_ref, table, acc, stage, p_buf, sems):
    phase, tile = pl.program_id(0), pl.program_id(1)
    col_nodes = table.shape[0]

    @pl.when(tile == 0)
    def _():
        def use(bufs, offset):
            for sub in range(0, p_buf.shape[1], 256):
                store_table(table, offset + sub, bufs[0][sub:sub + 256, :].astype(jnp.float32), 1)
        stream_rows([p_hbm], [p_buf], sems, phase * col_nodes, col_nodes, p_buf.shape[1], use)

    copy_rows(idx_ref, 0, idx_ref.shape[0], table, stage, 0, 1)
    for block in range(TILE_ROWS // LANES):
        total, = weighted_sum(stage, w_ref, block, 1)
        rows = pl.ds(pl.multiple_of(tile * TILE_ROWS + block * LANES, LANES), LANES)

        @pl.when(phase == 0)
        def _():
            acc[rows, :] = total

        @pl.when(phase > 0)
        def _():
            acc[rows, :] += total

    @pl.when(phase == pl.num_programs(0) - 1)
    def _():
        rows = pl.ds(pl.multiple_of(tile * TILE_ROWS, TILE_ROWS), TILE_ROWS)
        z_ref[...] = acc[rows, :]


def segment_kernel(width, n_src, build, chunks_ref, bounds_ref, idx_ref, col_ref, w_ref, *refs):
    sources, out_hbm = refs[:n_src], refs[n_src]
    table, acc, stage, sems, out_sem = refs[n_src + 1:n_src + 6]
    buffers = refs[n_src + 6:]
    phase, step = pl.program_id(0), pl.program_id(1)
    steps = pl.num_programs(1)

    @pl.when((phase == 0) & (step == 0))
    def _():
        def zero(n, carry):
            acc[pl.ds(pl.multiple_of(n * 256, 256), 256), :] = jnp.zeros((256, acc.shape[1]), jnp.float32)
            return carry
        lax.fori_loop(0, acc.shape[0] // 256, zero, 0)

    @pl.when(step == 0)
    def _():
        build(sources, buffers, sems, phase, table)

    for part in range(STEP_CHUNKS):
        chunk = step * STEP_CHUNKS + part

        @pl.when(chunk < chunks_ref[phase])
        def _():
            copy_rows(idx_ref, part * CHUNK, CHUNK, table, stage, 0, width)
            lanes = []
            for tile in range(width):
                rows = stage[pl.ds(tile, CHUNK, stride=width), :] if width > 1 else stage[...]
                lanes.append(rows.astype(jnp.bfloat16))
            gathered = jnp.concatenate(lanes, axis=1) if width > 1 else lanes[0]
            cols = col_ref[0, :, part * CHUNK:(part + 1) * CHUNK]
            weights = w_ref[0, :, part * CHUNK:(part + 1) * CHUNK]
            where = 2 * (phase * steps * STEP_CHUNKS + chunk)

            def body(block, carry):
                local = lax.broadcasted_iota(jnp.int32, (COL_TILE, CHUNK), 0) + block * COL_TILE
                select = jnp.where(local == cols, weights, 0.0).astype(jnp.bfloat16)
                at = pl.ds(pl.multiple_of(block * COL_TILE, COL_TILE), COL_TILE)
                acc[at, :] += jnp.dot(select, gathered, preferred_element_type=jnp.float32)
                return carry
            lax.fori_loop(bounds_ref[where], bounds_ref[where + 1] + 1, body, 0)

    @pl.when((phase == pl.num_programs(0) - 1) & (step == steps - 1))
    def _():
        copy = pltpu.make_async_copy(acc, out_hbm, out_sem)
        copy.start()
        copy.wait()


def build_plain(sources, buffers, sems, phase, table):
    rows = table.shape[0]

    def use(bufs, offset):
        for sub in range(0, bufs[0].shape[0], 256):
            store_table(table, offset + sub, bufs[0][sub:sub + 256, :].astype(jnp.float32), 1)
    stream_rows(sources, buffers, sems, phase * rows, rows, buffers[0].shape[1], use)


def build_dz(sources, buffers, sems, phase, table):
    z_hbm, b_hbm, w_out = sources
    rows = table.shape[0] // 2

    def use(bufs, offset):
        for sub in range(0, bufs[0].shape[0], 256):
            z_one = bufs[0][sub:sub + 256, :]
            back = bufs[1][sub:sub + 256, :]
            dh_one = lax.dot_general(back, w_out[...], CONTRACT_COLS, preferred_element_type=jnp.float32)
            dz_one = jnp.where(z_one.astype(jnp.float32) > 0, dh_one, 0.0).astype(jnp.bfloat16)
            store_table(table, offset + sub, dz_one.astype(jnp.float32), 2)
    stream_rows([z_hbm, b_hbm], buffers, sems, phase * rows, rows, buffers[0].shape[1], use)


def params():
    return pltpu.CompilerParams(vmem_limit_bytes=VMEM, dimension_semantics=("arbitrary", "arbitrary"))


def layer_one(idx, weights, x_all, w_hidden, w_out_pad):
    phases, slots, rows = weights.shape
    nodes, feat = x_all.shape
    tiles = rows // TILE_ROWS
    hid = w_hidden.shape[1]
    last = phases - 1
    whole = pl.BlockSpec(memory_space=pltpu.VMEM)
    return pl.pallas_call(
        layer_one_kernel,
        grid=(phases, tiles),
        in_specs=[
            pl.BlockSpec((slots * TILE_ROWS,), lambda k, t: (k * tiles + t,), memory_space=pltpu.SMEM),
            pl.BlockSpec((1, slots, TILE_ROWS), lambda k, t: (k, 0, t)),
            pl.BlockSpec(memory_space=pl.ANY), whole, whole],
        out_specs=[
            pl.BlockSpec((TILE_ROWS, hid), lambda k, t: (jnp.where(k == last, t, 0), 0)),
            pl.BlockSpec((TILE_ROWS, LANES), lambda k, t: (jnp.where(k == last, t, 0), 0))],
        out_shape=[jax.ShapeDtypeStruct((rows, hid), jnp.bfloat16), jax.ShapeDtypeStruct((rows, LANES), jnp.bfloat16)],
        scratch_shapes=[
            pltpu.VMEM((2 * nodes // phases, LANES), jnp.float32), pltpu.VMEM((rows, hid), jnp.float32),
            pltpu.VMEM((2 * slots * TILE_ROWS, LANES), jnp.float32), pltpu.VMEM((2, 2048, feat), jnp.bfloat16),
            pltpu.SemaphoreType.DMA((1, 2))],
        compiler_params=params(),
        cost_estimate=pl.CostEstimate(flops=3 * 10**11, bytes_accessed=10**8, transcendentals=0),
        name="layer_one")(idx, weights, x_all, w_hidden, w_out_pad)


def layer_two(idx, weights, p_all):
    phases, slots, rows = weights.shape
    tiles = rows // TILE_ROWS
    last = phases - 1
    return pl.pallas_call(
        layer_two_kernel,
        grid=(phases, tiles),
        in_specs=[
            pl.BlockSpec((slots * TILE_ROWS,), lambda k, t: (k * tiles + t,), memory_space=pltpu.SMEM),
            pl.BlockSpec((1, slots, TILE_ROWS), lambda k, t: (k, 0, t)),
            pl.BlockSpec(memory_space=pl.ANY)],
        out_specs=pl.BlockSpec((TILE_ROWS, LANES), lambda k, t: (jnp.where(k == last, t, 0), 0)),
        out_shape=jax.ShapeDtypeStruct((rows, LANES), jnp.float32),
        scratch_shapes=[
            pltpu.VMEM((p_all.shape[0] // phases, LANES), jnp.float32), pltpu.VMEM((rows, LANES), jnp.float32),
            pltpu.VMEM((slots * TILE_ROWS, LANES), jnp.float32), pltpu.VMEM((2, 2048, LANES), jnp.bfloat16),
            pltpu.SemaphoreType.DMA((1, 2))],
        compiler_params=params(),
        cost_estimate=pl.CostEstimate(flops=3 * 10**11, bytes_accessed=10**8, transcendentals=0),
        name="layer_two")(idx, weights, p_all)


def segment_product(name, build, chunks, bounds, idx, cols, weights, sources, specs, buffers, num_out, width, rows):
    phases, edges = cols.shape
    per_step = CHUNK * STEP_CHUNKS
    steps = edges // per_step
    tile_spec = pl.BlockSpec((1, 1, per_step), lambda p, t, *_: (p * steps + t, 0, 0))
    grid_spec = pltpu.PrefetchScalarGridSpec(
        num_scalar_prefetch=2,
        grid=(phases, steps),
        in_specs=[pl.BlockSpec((per_step,), lambda p, t, *_: (p * steps + t,), memory_space=pltpu.SMEM),
                  tile_spec, tile_spec, *specs],
        out_specs=pl.BlockSpec(memory_space=pl.ANY),
        scratch_shapes=[
            pltpu.VMEM((width * rows, LANES), jnp.float32), pltpu.VMEM((num_out, width * LANES), jnp.float32),
            pltpu.VMEM((width * CHUNK, LANES), jnp.float32), pltpu.SemaphoreType.DMA((len(buffers), 2)),
            pltpu.SemaphoreType.DMA, *buffers])
    return pl.pallas_call(
        functools.partial(segment_kernel, width, len(sources), build),
        grid_spec=grid_spec,
        out_shape=jax.ShapeDtypeStruct((num_out, width * LANES), jnp.float32),
        compiler_params=params(),
        cost_estimate=pl.CostEstimate(flops=3 * 10**11, bytes_accessed=10**8, transcendentals=0),
        name=name)(chunks, bounds, (idx * width).reshape(-1), cols.reshape(phases * steps, 1, per_step),
                   weights.reshape(phases * steps, 1, per_step), *sources)


def solution(mesh):
    row_size = mesh.shape["row"]
    col_size = mesh.shape["col"]
    both_axes = ("row", "col")
    swap = [(0, 1), (1, 0)]

    def device_step(feat_blk, w_hidden, w_output, cols_blk, vals_blk, mask_blk, labels_blk, train_blk):
        row_i, col_j = lax.axis_index("row"), lax.axis_index("col")
        blk_nodes = feat_blk.shape[0]
        col_nodes = blk_nodes * row_size
        slots = cols_blk.shape[0]
        classes = w_output.shape[1]
        any_spec = pl.BlockSpec(memory_space=pl.ANY)
        whole = pl.BlockSpec(memory_space=pltpu.VMEM)
        weights = vals_blk.astype(jnp.float32) * mask_blk.astype(jnp.float32)
        w_out_pad = jnp.pad(w_output, ((0, 0), (0, LANES - classes)))

        x_all = lax.all_gather(feat_blk, both_axes, axis=0, tiled=True)
        own_cols = lax.all_to_all(cols_blk, "col", split_axis=1, concat_axis=0, tiled=True)
        own_w = lax.all_to_all(vals_blk * mask_blk.astype(jnp.bfloat16), "col", split_axis=1, concat_axis=0, tiled=True)
        own_w = own_w.astype(jnp.float32).reshape(col_size, slots, blk_nodes)
        own_cols = own_cols.reshape(col_size, slots, blk_nodes // TILE_ROWS, TILE_ROWS).transpose(0, 2, 1, 3).reshape(-1)

        first_half = 1 - row_i
        turned = jnp.bitwise_xor(cols_blk, first_half * blk_nodes)
        row_ids = lax.broadcasted_iota(jnp.int32, (slots, col_size, blk_nodes), 2)
        valid = mask_blk.reshape(slots, col_size, blk_nodes) > 0
        keys = jnp.where(valid, turned.reshape(slots, col_size, blk_nodes), col_nodes) * blk_nodes + row_ids
        keys = keys.transpose(1, 0, 2).reshape(col_size, slots * blk_nodes)
        edge_w = weights.reshape(slots, col_size, blk_nodes).transpose(1, 0, 2).reshape(col_size, slots * blk_nodes)
        keys, edge_w = lax.sort((keys, edge_w), dimension=1, num_keys=1, is_stable=False)
        edge_cols, edge_rows = keys // blk_nodes, keys % blk_nodes
        chunked = edge_cols.reshape(col_size, -1, CHUNK)
        low = chunked[:, :, 0] // COL_TILE
        high = jnp.max(jnp.where(chunked < col_nodes, chunked, 0), axis=2) // COL_TILE
        bounds = jnp.stack([low, high], axis=2).reshape(-1)
        chunks = jnp.sum((chunked[:, :, 0] < col_nodes).astype(jnp.int32), axis=1)

        z_one, proj_two = layer_one(own_cols * 2, own_w, x_all, w_hidden, w_out_pad)
        p_all = lax.all_gather(proj_two, both_axes, axis=0, tiled=True)
        z_all = lax.all_gather(z_one, "col", axis=0, tiled=True)
        z_two = layer_two(own_cols, own_w, p_all)[:, :classes]

        mask_f = train_blk.astype(jnp.float32)
        train_count = jnp.maximum(lax.psum(jnp.sum(train_blk), both_axes), 1).astype(jnp.float32)
        log_norm = jax.nn.logsumexp(z_two, axis=1)
        onehot = (labels_blk[:, None] == jnp.arange(classes, dtype=jnp.int32)[None, :]).astype(jnp.float32)
        picked = jnp.sum(z_two * onehot, axis=1)
        loss_mean = lax.psum(jnp.sum(mask_f * (log_norm - picked)), both_axes) / train_count
        softmax_z = jnp.exp(z_two - log_norm[:, None])
        grad_two = ((mask_f / train_count)[:, None] * (softmax_z - onehot)).astype(jnp.bfloat16)
        grad_two = jnp.pad(grad_two, ((0, 0), (0, LANES - classes)))
        grad_rows = lax.all_gather(grad_two, "col", axis=0, tiled=True)

        part_two = segment_product(
            "back_two", build_plain, chunks, bounds, edge_rows, edge_cols, edge_w, [grad_rows], [any_spec],
            [pltpu.VMEM((2, 2048, LANES), jnp.bfloat16)], col_nodes, 1, blk_nodes)
        other = lax.ppermute(part_two[:blk_nodes], "row", swap)
        back_two = (part_two[blk_nodes:] + other).astype(jnp.bfloat16)
        back_all = lax.all_gather(back_two, ("col", "row"), axis=0, tiled=True)
        back_rows = lax.dynamic_slice_in_dim(back_all, row_i * col_size * blk_nodes, col_size * blk_nodes, 0)
        back_own = lax.dynamic_slice_in_dim(back_rows, col_j * blk_nodes, blk_nodes, 0)
        h_one = jnp.maximum(z_one, 0)
        grad_w_output = lax.dot_general(h_one, back_own, CONTRACT_ROWS, preferred_element_type=jnp.float32)[:, :classes]

        part_one = segment_product(
            "back_one", build_dz, chunks, bounds, edge_rows, edge_cols, edge_w, [z_all, back_rows, w_out_pad],
            [any_spec, any_spec, whole],
            [pltpu.VMEM((2, 1024, 2 * LANES), jnp.bfloat16), pltpu.VMEM((2, 1024, LANES), jnp.bfloat16)],
            col_nodes, 2, blk_nodes)
        other = lax.ppermute(part_one[:blk_nodes], "row", swap)
        back_one = (part_one[blk_nodes:] + other).astype(jnp.bfloat16)
        feat_src = lax.dynamic_slice_in_dim(x_all, (col_j * row_size + row_i) * blk_nodes, blk_nodes, 0)
        grad_w_hidden = lax.dot_general(feat_src, back_one, CONTRACT_ROWS, preferred_element_type=jnp.float32)
        grad_w_hidden = lax.psum(grad_w_hidden, both_axes)
        grad_w_output = lax.psum(grad_w_output, both_axes)
        return loss_mean, grad_w_hidden, grad_w_output

    node_spec = P(("row", "col"), None)
    label_spec = P(("row", "col"))
    adj_spec = P("col", "row")
    return jax.shard_map(device_step, mesh=mesh, in_specs=(node_spec, P(), P(), adj_spec, adj_spec, adj_spec, label_spec, label_spec), out_specs=(P(), P(), P()), check_vma=False)
```

time: 7100 us -> 3260 us (0.46)
  other arithmetic: 3540 us -> 230 us
  Pallas kernels: 0 us -> 2100 us
  local copies, waits for them, and re-layouts: 1940 us -> 52 us
  waiting for transfers between devices: 1500 us -> 769 us
    scatter-add x8 -> x0, other arithmetic: 3190 us -> none  [slot_step(): jax.ops.segment_sum(slot_w[:, None] * dense, col_ids, num_segments=num_out)]
    pallas_call x0 -> x4, Pallas kernels: none -> 2100 us  [the longest x2 1150 us: segment_product(): pl.pallas_call(functools.partial(segment_kernel, width, len(sources), bui...]
    gather x8 -> x0, local copies, waits for them, and re-layouts: 1900 us -> none  [slot_step(): return (running + slot_w[:, None] * jnp.take(dense, col_ids, axis=0), None)]
    unnamed x10 -> x6, waiting for transfers between devices: 554 us -> 1.28 us
    add x8 -> x1, other arithmetic: 318 us -> 0.19 us  [device_step(): jnp.where(valid, turned.reshape(slots, col_size, blk_nodes), col_nodes)]
    reduce_scatter x3 -> x0, waiting for transfers between devices: 308 us -> none  [the longest x1 259 us: device_step(): z_two = lax.psum_scatter(part_two, 'col', scatter_dimension=0, tiled=True)]
    all_gather x3 -> x4, waiting for transfers between devices: 472 us -> 687 us  [the longest x1 279 us: device_step(): z_all = lax.all_gather(z_one, 'col', axis=0, tiled=True)]
    sort x0 -> x1, other arithmetic: none -> 191 us  [device_step(): lax.sort((keys, edge_w), dimension=1, num_keys=1, is_stable=False)]
  transfers between devices with their start and end apart: 12 -> 10, of which waited for: 9 -> 9; matrix products, arithmetic and copies ran while one was open for 0% -> 7% of each run, Pallas kernels for 0% -> 0%
where the time goes in v1:
time: 3260 us; the launch traced here: 3240 us
  Pallas kernels  2100 us (64%)
  waiting for transfers between devices  769 us (24%)
  other arithmetic  230 us (7%)
  local copies, waits for them, and re-layouts  52 us (2%)
  blocking collectives  46.2 us (1%)
    pallas_call x2, Pallas kernels, segment_product(): pl.pallas_call(functools.partial(segment_kernel, width, len(sources), bui...  1150 us
    pallas_call x1, Pallas kernels, layer_one(): pl.pallas_call(layer_one_kernel, grid=(phases, tiles), in_specs=[pl.Block...  476 us
    pallas_call x1, Pallas kernels, layer_two(): pl.pallas_call(layer_two_kernel, grid=(phases, tiles), in_specs=[pl.Block...  467 us
    all_gather x1, waiting for transfers between devices, device_step(): z_all = lax.all_gather(z_one, 'col', axis=0, tiled=True)  279 us
    sort x1, other arithmetic, device_step(): lax.sort((keys, edge_w), dimension=1, num_keys=1, is_stable=False)  191 us
    all_gather x1, waiting for transfers between devices, device_step(): back_all = lax.all_gather(back_two, ('col', 'row'), axis=0, tiled=True)  153 us
    all_gather x1, waiting for transfers between devices, device_step(): p_all = lax.all_gather(proj_two, both_axes, axis=0, tiled=True)  132 us
    all_gather x1, waiting for transfers between devices, device_step(): x_all = lax.all_gather(feat_blk, both_axes, axis=0, tiled=True)  123 us
  transfers between devices with their start and end apart: 10, of which 9 were waited for; matrix products, arithmetic and copies ran while one was open for 7% of the time, Pallas kernels for 0%

profile of v1, /device:TPU:0, one launch (start us, length us, event | category | flops | bytes accessed | tf_op | source)
XLA Modules:
  0.0 3241.4 jit_solution(9372935135895896063)
XLA Ops:
  7.2 0.7 all-gather.6.cloned.1.call-update
  7.9 2.5 convert_multiply_fusion.1
  10.4 5.6 all-to-all-start.1
  16.0 0.8 copy.33
  16.8 0.7 pad.8.w_output.refs_2_
  17.5 6.3 all-to-all-done.1
  23.7 3.5 all-to-all-start
  27.3 0.0 all-gather.8.cloned.1.call-start
  27.3 1.1 convert_bitcast_fusion.w_ref
  28.4 24.2 all-to-all-done
  52.5 0.7 reshape.122
  53.3 0.7 copy.32
  53.9 0.3 copy.38
  54.2 1.0 copy-done.4
  55.2 1.0 broadcast_multiply_fusion.idx_ref
  56.3 122.8 %all-gather.6.cloned.1.call-done.x_hbm = bf16[131072,128]{1,0:T(8,128)(2,1)} async-done(((bf16[16384,128]{1,0:T(8,128)(2,1)}), bf16[131072,128]{1,0:T(8,128)(2,1)}) %all-gather.6.cloned.1.call-update) | async-done | bytes 33554448 | tf_op jit(solution)/shard_map/all_gather | solution.py:319
  179.1 475.9 %layer_one.1 = (bf16[16384,256]{1,0:T(8,128)(2,1)}, bf16[16384,128]{1,0:T(8,128)(2,1)}) custom-call(s32[262144]{0:T(1024)} %broadcast_multiply_fusion.idx_ref, f32[4,4,16384]{2,1,0:T(4,128)} %convert_bitcast_fusion.w_ref, bf16[131072,128]{1,0:T(8,128)(2,1)} %all-gather.6.cloned.1.call-done.x_hbm, bf16[128,256]{1,0:T(8,128)(2,1)} %w_hidden.1, ...), custom_call_target="tpu_custom_call" | custom-call | flops 299999985664 | bytes 100000000 | tf_op jit(solution)/shard_map/layer_one/pallas_call | solution.py:235
  655.1 0.0 all-gather.12.cloned.1.call-start
  655.1 0.6 reduce_sum.48
  655.8 23.0 psum.29
  679.4 131.8 %all-gather.8.cloned.1.call-done.p_hbm = bf16[131072,128]{1,0:T(8,128)(2,1)} async-done(((bf16[16384,128]{1,0:T(8,128)(2,1)}), bf16[131072,128]{1,0:T(8,128)(2,1)}) %all-gather.8.cloned.1.call-update) | async-done | bytes 33554448 | tf_op jit(solution)/shard_map/all_gather | solution.py:341
  811.2 467.4 %layer_two.1 = f32[16384,128]{1,0:T(8,128)} custom-call(s32[262144]{0:T(1024)} %bitcast.31, f32[4,4,16384]{2,1,0:T(4,128)} %convert_bitcast_fusion.w_ref, bf16[131072,128]{1,0:T(8,128)(2,1)} %all-gather.8.cloned.1.call-done.p_hbm), custom_call_target="tpu_custom_call" | custom-call | flops 299999985664 | bytes 100000000 | tf_op jit(solution)/shard_map/layer_two/pallas_call | solution.py:259
  1278.7 5.4 slice_reduce_fusion
  1284.1 0.4 copy-done
  1284.5 10.2 select_reduce_fusion
  1294.8 0.6 multiply_reduce_fusion
  1295.4 7.8 multiply_convert_fusion
  1303.2 2.5 pad.9
  1305.7 0.0 all-gather.14.cloned.1.call-start
  1305.8 0.4 select_multiply_fusion
  1306.2 0.9 mul.67
  1307.1 1.3 convert_multiply_fusion
  1308.4 0.9 reshape.125
  1309.3 0.2 iota_add_fusion
  1309.5 190.5 %sort.15 = (s32[4,65536]{1,0:T(4,128)}, f32[4,65536]{1,0:T(4,128)S(1)}) sort(s32[4,65536]{1,0:T(4,128)S(1)} %bitcast.34, f32[4,65536]{1,0:T(4,128)S(1)} %bitcast.33), dimensions={1}, to_apply=%region_7.8 | sort | flops 4718592 | bytes 4194304 | tf_op jit(solution)/shard_map/sort | solution.py:332
  1500.0 2.5 reshape.131.w_ref
  1502.5 4.1 multiply_bitcast_fusion
  1506.6 2.4 reshape.130.col_ref
  1509.0 0.2 copy.45
  1509.2 0.4 fusion.9
  1509.5 0.2 copy.34
  1509.8 1.1 copy.41
  1510.8 0.3 add_select_fusion.2
  1511.1 1.0 add_select_fusion.3
  1512.1 0.2 pad_add_fusion
  1512.3 0.9 reshape.128.bounds_ref
  1513.2 535.8 %back_two.1 = f32[32768,128]{1,0:T(8,128)} custom-call(s32[4]{0:T(128)} %get-tuple-element.21.chunks_ref, s32[2048]{0:T(1024)} %reshape.128.bounds_ref, s32[262144]{0:T(1024)} %bitcast.39, s32[256,1,1024]{2,1,0:T(1,128)} %reshape.130.col_ref, f32[256,1,1024]{2,1,0:T(1,128)} %reshape.131.w_ref, bf16[65536,128]{1,0:T(8,128)(2,1)} %all-gather.12.cloned.1.call-done.refs_0_), custom_call_target="tpu_custom_call" | custom-call | flops 299999985664 | bytes 100000000 | tf_op jit(solution)/shard_map/back_two/pallas_call | solution.py:292
  2049.0 7.6 slice.33
  2056.6 13.2 collective-permute-done
  2069.7 2.3 fusion.3
  2072.2 0.5 all-gather.10.cloned.1.call-update
  2072.8 0.6 copy-done.5
  2073.3 1.0 copy.40
  2074.4 153.2 %all-gather.14.cloned.1.call-done = bf16[131072,128]{1,0:T(8,128)(2,1)} async-done(((bf16[16384,128]{1,0:T(8,128)(2,1)}), bf16[131072,128]{1,0:T(8,128)(2,1)}) %all-gather.14.cloned.1.call-update) | async-done | bytes 33554448 | tf_op jit(solution)/shard_map/all_gather | solution.py:361
  2227.5 14.0 constant_dynamic-slice_fusion.refs_1_
  2241.5 279.3 %all-gather.10.cloned.1.call-done.refs_0_ = bf16[65536,256]{1,0:T(8,128)(2,1)} async-done(((bf16[16384,256]{1,0:T(8,128)(2,1)}), bf16[65536,256]{1,0:T(8,128)(2,1)}) %all-gather.10.cloned.1.call-update) | async-done | bytes 33554448 | tf_op jit(solution)/shard_map/all_gather | solution.py:342
  2520.8 617.8 %back_one.1 = f32[32768,256]{1,0:T(8,128)} custom-call(s32[4]{0:T(128)} %get-tuple-element.21.chunks_ref, s32[2048]{0:T(1024)} %reshape.128.bounds_ref, s32[262144]{0:T(1024)} %bitcast.38, s32[256,1,1024]{2,1,0:T(1,128)} %reshape.130.col_ref, f32[256,1,1024]{2,1,0:T(1,128)} %reshape.131.w_ref, bf16[65536,256]{1,0:T(8,128)(2,1)} %all-gather.10.cloned.1.call-done.refs_0_, ...), custom_call_target="tpu_custom_call" | custom-call | flops 299999985664 | bytes 100000000 | tf_op jit(solution)/shard_map/back_one/pallas_call | solution.py:292
  3138.5 11.3 slice.35
  3149.8 25.1 collective-permute-done.1
  3174.9 14.3 fusion.1
  3189.2 6.5 fusion.4
  3195.7 23.2 all-reduce.2
  3219.6 11.8 all-reduce.5.cloned.1.call-done
  3231.4 1.6 copy.47
  (26 shorter events, 0.2 us)
Async XLA Ops:
  7.2 171.9 %all-gather.6.cloned.1.call-start = ((), (), s32[]{:S(2)}) async-start(), calls=%async_computation.2 | async-start | bytes 37748736 | tf_op jit(solution)/shard_map/all_gather | solution.py:319
  10.4 13.3 all-to-all-start.1
  23.7 28.8 all-to-all-start
  27.3 784.0 %all-gather.8.cloned.1.call-start = ((), (), s32[]{:S(2)}) async-start(), calls=%async_computation.3 | async-start | bytes 37748736 | tf_op jit(solution)/shard_map/all_gather | solution.py:341
  54.2 1.0 copy-start.4
  179.1 476.0 %copy-start.7 = (s32[16384]{0:T(1024)S(1)}, s32[16384]{0:T(1024)}, u32[]{:S(2)}) copy-start(s32[16384]{0:T(1024)} %param.15) | copy-start | bytes 196612
  655.1 858.1 %all-gather.12.cloned.1.call-start = ((), (), s32[]{:S(2)}) async-start(), calls=%async_computation.5 | async-start | bytes 20971520 | tf_op jit(solution)/shard_map/all_gather | solution.py:354
  1278.7 5.8 copy-start
  1278.7 5.8 copy-start.6
  1278.7 16.1 copy-start.8
  1303.2 2.6 copy-start.2
  1303.2 2.6 copy-start.3
  1305.7 921.8 %all-gather.14.cloned.1.call-start = ((), (), s32[]{:S(2)}) async-start(), calls=%async_computation.6 | async-start | bytes 37748736 | tf_op jit(solution)/shard_map/all_gather | solution.py:361
  2049.0 20.7 copy-start.1
  2056.6 13.2 collective-permute-start
  2072.1 1.2 copy-start.5
  2072.1 448.6 %all-gather.10.cloned.1.call-start = ((), (), s32[]{:S(2)}) async-start(), calls=%async_computation.4 | async-start | bytes 41943040 | tf_op jit(solution)/shard_map/all_gather | solution.py:342
  2072.7 1158.7 %all-reduce.5.cloned.1.call-start = ((), (), s32[]{:S(2)}) async-start(), calls=%async_computation.7 | async-start | bytes 262144 | tf_op jit(solution)/shard_map/psum | solution.py:376
  3149.8 25.1 collective-permute-start.1
Sparse Core Ops, SparseCore 0:
  9.8 169.2 all-gather.5
  655.2 155.9 all-gather.7
  1305.8 151.8 all-gather.11
  2072.2 155.2 all-gather.13
  2229.2 291.5 all-gather.9
  3189.3 42.0 all-reduce.4

commit v2 on v1

v2 whole, which is shorter than its diff:
```python
import functools

import jax
import jax.numpy as jnp
from jax import lax
from jax.experimental import pallas as pl
from jax.experimental.pallas import tpu as pltpu
from jax.sharding import PartitionSpec as P

CONTRACT_ROWS = (((0,), (0,)), ((), ()))
CONTRACT_COLS = (((1,), (1,)), ((), ()))
LANES = 128
SUB_ROWS = 256
STEP_SUBS = 4
BUF_SUBS = 2
CHUNK = 256
BUF_CHUNKS = 4
STEP_CHUNKS = 8
WINDOW = 256
PACK = 3
VMEM = 60 << 20


def copy_row(ids, e, table, stage, at, width):
    if width == 1:
        stage[at, :] = table[ids[e], :]
    else:
        stage[width * at:width * (at + 1), :] = table[pl.ds(pl.multiple_of(ids[e], width), width), :]


def index_copy(idx_hbm, ids, sems, buf, step):
    size = ids[buf].shape[0]
    start = pl.multiple_of((step * len(ids) + buf) * size, size)
    return pltpu.make_async_copy(idx_hbm.at[pl.ds(start, size)], ids[buf], sems.at[buf])


def start_next(idx_hbm, ids, sems, buf, step, total):
    @pl.when(step + 1 < total)
    def _():
        index_copy(idx_hbm, ids, sems, buf, step + 1).start()


def store_table(table, first, value, width):
    rows = value.shape[0]
    for part in range(width):
        piece = value[:, part * LANES:(part + 1) * LANES]
        if width == 1:
            table[pl.ds(pl.multiple_of(first, rows), rows), :] = piece
        else:
            table[pl.ds(width * first + part, rows, stride=width), :] = piece


def stream_rows(sources, buffers, sems, first_row, total, chunk, use, sem_row=0):
    steps = total // chunk

    def copies(step, slot):
        start = pl.multiple_of(first_row + step * chunk, chunk)
        return [pltpu.make_async_copy(src.at[pl.ds(start, chunk), :], buf.at[slot], sems.at[sem_row + n, slot])
                for n, (src, buf) in enumerate(zip(sources, buffers))]
    for c in copies(0, 0):
        c.start()

    def body(step, carry):
        slot = lax.rem(step, 2)
        for c in copies(step, slot):
            c.wait()

        @pl.when(step + 1 < steps)
        def _():
            for c in copies(step + 1, 1 - slot):
                c.start()
        use([buf.at[slot] for buf in buffers], step * chunk)
        return carry
    lax.fori_loop(0, steps, body, 0)


def weighted_sum(stage, w_ref, sub, block, width):
    slots = w_ref.shape[1]
    first = sub * SUB_ROWS + block * LANES
    w_rows = w_ref[0, :, first:first + LANES]
    w_cols = jnp.concatenate([w_rows] * (8 // slots), axis=0).T
    parts = [None] * width
    for slot in range(slots):
        column = jnp.broadcast_to(w_cols[:, slot:slot + 1], (LANES, LANES))
        at = width * (slot * SUB_ROWS + block * LANES)
        for part in range(width):
            rows = stage[pl.ds(at + part, LANES, stride=width), :] if width > 1 else stage[at:at + LANES, :]
            term = column * rows
            parts[part] = term if slot == 0 else parts[part] + term
    return parts


def forward_step(idx_hbm, w_ref, table, acc, ids, stages, idx_sems, width):
    phase, tile = pl.program_id(0), pl.program_id(1)
    step = phase * pl.num_programs(1) + tile
    total = pl.num_programs(0) * pl.num_programs(1)
    slots = w_ref.shape[1]
    blocks = SUB_ROWS // LANES
    first_row = tile * STEP_SUBS * SUB_ROWS

    @pl.when(step == 0)
    def _():
        for buf in range(len(ids)):
            index_copy(idx_hbm, ids, idx_sems, buf, step).start()

    def add(sub, block):
        parts = weighted_sum(stages[sub % len(stages)], w_ref, sub, block, width)
        rows = pl.ds(pl.multiple_of(first_row + sub * SUB_ROWS + block * LANES, LANES), LANES)
        for part in range(width):
            acc[rows, part * LANES:(part + 1) * LANES] += parts[part]

    @pl.when(phase == 0)
    def _():
        rows = pl.ds(pl.multiple_of(first_row, STEP_SUBS * SUB_ROWS), STEP_SUBS * SUB_ROWS)
        acc[rows, :] = jnp.zeros((STEP_SUBS * SUB_ROWS, acc.shape[1]), jnp.float32)

    edges = slots * SUB_ROWS
    for sub in range(STEP_SUBS):
        buf, part = sub // BUF_SUBS, sub % BUF_SUBS
        if part == 0:
            index_copy(idx_hbm, ids, idx_sems, buf, step).wait()
        for block in range(blocks):
            for e in range(block * edges // blocks, (block + 1) * edges // blocks):
                copy_row(ids[buf], part * edges + e, table, stages[sub % len(stages)], e, width)
            if sub > 0:
                add(sub - 1, block)
        if part == BUF_SUBS - 1:
            start_next(idx_hbm, ids, idx_sems, buf, step, total)
    for block in range(blocks):
        add(STEP_SUBS - 1, block)


def layer_one_kernel(idx_hbm, w_ref, x_hbm, w_hidden, w_output, z_ref, p_ref, table, acc, ids_a, ids_b, stage_a, stage_b, x_buf,
                     sems, idx_sems):
    phase, tile = pl.program_id(0), pl.program_id(1)
    col_nodes = table.shape[0] // 2

    @pl.when(tile == 0)
    def _():
        def use(bufs, offset):
            for sub in range(0, x_buf.shape[1], 256):
                proj = jnp.dot(bufs[0][sub:sub + 256, :], w_hidden[...], preferred_element_type=jnp.float32)
                proj = proj.astype(jnp.bfloat16).astype(jnp.float32)
                store_table(table, offset + sub, proj, 2)
        stream_rows([x_hbm], [x_buf], sems, phase * col_nodes, col_nodes, x_buf.shape[1], use)

    forward_step(idx_hbm, w_ref, table, acc, [ids_a, ids_b], [stage_a, stage_b], idx_sems, 2)

    @pl.when(phase == pl.num_programs(0) - 1)
    def _():
        size = STEP_SUBS * SUB_ROWS
        z_one = acc[pl.ds(pl.multiple_of(tile * size, size), size), :].astype(jnp.bfloat16)
        z_ref[...] = z_one
        h_one = jnp.maximum(z_one, 0)
        p_ref[...] = jnp.dot(h_one, w_output[...], preferred_element_type=jnp.float32).astype(jnp.bfloat16)


def unpack_table(table, p_hbm, p_buf, sems, first_block, blocks, nodes, sem_row=0):
    chunk = p_buf.shape[1]
    packed = packed_rows(nodes)
    for block in range(blocks):
        def use(bufs, offset):
            value = bufs[0][...].astype(jnp.float32)
            for q in range(PACK):
                turned = value if q == 0 else pltpu.roll(value, LANES - q * pack_lanes(), 1)
                first = pl.multiple_of(block * nodes + q * packed + offset, 16)
                table[pl.ds(first, chunk), :] = turned.astype(table.dtype)
        stream_rows([p_hbm], [p_buf], sems, (first_block + block) * packed, packed, chunk, use, sem_row)


def pack_lanes():
    return LANES // PACK // 8 * 8


def packed_rows(nodes):
    return -(-nodes // (PACK * 96)) * 96


def pack_nodes(values):
    nodes = values.shape[0]
    packed = packed_rows(nodes)
    values = jnp.pad(values, ((0, PACK * packed - nodes), (0, pack_lanes() - values.shape[1])))
    parts = [values[q * packed:(q + 1) * packed] for q in range(PACK)]
    return jnp.pad(jnp.concatenate(parts, axis=1), ((0, 0), (0, LANES - PACK * pack_lanes())))


def layer_two_kernel(nodes, idx_hbm, w_ref, p_hbm, z_ref, table, acc, ids_a, ids_b, stage_a, stage_b, p_buf, sems, idx_sems):
    phase, tile = pl.program_id(0), pl.program_id(1)

    @pl.when(tile == 0)
    def _():
        unpack_table(table, p_hbm, p_buf, sems, phase * 2, 2, nodes)

    forward_step(idx_hbm, w_ref, table, acc, [ids_a, ids_b], [stage_a, stage_b], idx_sems, 1)

    @pl.when(phase == pl.num_programs(0) - 1)
    def _():
        size = STEP_SUBS * SUB_ROWS
        z_ref[...] = acc[pl.ds(pl.multiple_of(tile * size, size), size), :]


def segment_kernel(width, n_src, build, active_ref, over_ref, base_ref, last_ref, idx_hbm, col_ref, w_ref, *refs):
    sources, out_hbm = refs[:n_src], refs[n_src]
    table, acc, ids_a, ids_b, ids_c, stage_a, stage_b, sems, idx_sems, out_sem = refs[n_src + 1:n_src + 11]
    buffers = refs[n_src + 11:]
    ids, stages = [ids_a, ids_b], [stage_a, stage_b]
    phase, tile = pl.program_id(0), pl.program_id(1)
    steps = pl.num_programs(1)
    step = phase * steps + tile
    total = pl.num_programs(0) * steps

    @pl.when(step == 0)
    def _():
        for buf in range(len(ids)):
            index_copy(idx_hbm, ids, idx_sems, buf, step).start()

        def zero(n, carry):
            acc[pl.ds(pl.multiple_of(n * 256, 256), 256), :] = jnp.zeros((256, acc.shape[1]), jnp.float32)
            return carry
        lax.fori_loop(0, acc.shape[0] // 256, zero, 0)

    @pl.when(tile == 0)
    def _():
        build(sources, buffers, sems, phase, table)

    def gathered(stage):
        lanes = []
        for part in range(width):
            rows = stage[pl.ds(part, CHUNK, stride=width), :] if width > 1 else stage[...]
            lanes.append(rows.astype(jnp.bfloat16))
        return jnp.concatenate(lanes, axis=1) if width > 1 else lanes[0]

    def product(cols, weights, rows, base):
        local = lax.broadcasted_iota(jnp.int32, (WINDOW, CHUNK), 0)
        select = jnp.where(local == cols - base, weights, 0.0).astype(jnp.bfloat16)
        acc[pl.ds(pl.multiple_of(base, 8), WINDOW), :] += jnp.dot(select, rows, preferred_element_type=jnp.float32)

    def add(chunk):
        part = slice(chunk * CHUNK, (chunk + 1) * CHUNK)
        base = base_ref[step * STEP_CHUNKS + chunk]
        product(col_ref[0, :, part], w_ref[0, :, part], gathered(stages[chunk % 2]), base)

    active = tile < active_ref[phase]

    @pl.when(active)
    def _():
        for chunk in range(STEP_CHUNKS):
            buf, part = chunk // BUF_CHUNKS, chunk % BUF_CHUNKS
            if part == 0:
                index_copy(idx_hbm, ids, idx_sems, buf, step).wait()
            for e in range(CHUNK):
                copy_row(ids[buf], part * CHUNK + e, table, stages[chunk % 2], e, width)
            if chunk > 0:
                add(chunk - 1)
            if part == BUF_CHUNKS - 1:
                start_next(idx_hbm, ids, idx_sems, buf, step, total)
        add(STEP_CHUNKS - 1)

    @pl.when(jnp.logical_not(active))
    def _():
        for buf in range(len(ids)):
            index_copy(idx_hbm, ids, idx_sems, buf, step).wait()
            start_next(idx_hbm, ids, idx_sems, buf, step, total)

    @pl.when(active & (over_ref[step] > 0))
    def _():
        size = STEP_CHUNKS * CHUNK
        copy = pltpu.make_async_copy(idx_hbm.at[pl.ds(pl.multiple_of(step * size, size), size)], ids_c, out_sem)
        copy.start()
        copy.wait()
        for chunk in range(STEP_CHUNKS):
            base, last = base_ref[step * STEP_CHUNKS + chunk], last_ref[step * STEP_CHUNKS + chunk]

            @pl.when(last >= base + WINDOW)
            def _():
                def fetch(e, carry):
                    copy_row(ids_c, chunk * CHUNK + e, table, stage_a, 0, width)
                    if width == 1:
                        stage_b[pl.ds(e, 1), :] = stage_a[0:1, :]
                    else:
                        stage_b[pl.ds(width * e, width), :] = stage_a[0:width, :]
                    return carry
                lax.fori_loop(0, CHUNK, fetch, 0)
                part = slice(chunk * CHUNK, (chunk + 1) * CHUNK)
                cols, weights = col_ref[0, :, part], w_ref[0, :, part]
                rows = gathered(stage_b)
                end = acc.shape[0] - WINDOW

                def more(window, carry):
                    start = base + window * WINDOW
                    fresh = jnp.where(cols >= start, weights, 0.0)
                    product(cols, fresh, rows, jnp.minimum(start, end))
                    return carry
                lax.fori_loop(1, (last - base) // WINDOW + 1, more, 0)

    @pl.when(step == total - 1)
    def _():
        copy = pltpu.make_async_copy(acc, out_hbm, out_sem)
        copy.start()
        copy.wait()


def build_packed(nodes, sources, buffers, sems, phase, table):
    unpack_table(table, sources[0], buffers[0], sems, phase, 1, nodes)


def build_dz(nodes, sources, buffers, sems, phase, table):
    z_hbm, b_hbm, w_out = sources
    z_buf, b_buf, back = buffers
    unpack_table(back, b_hbm, b_buf, sems, phase, 1, nodes, 1)

    def use(bufs, offset):
        for sub in range(0, z_buf.shape[1], 256):
            z_one = bufs[0][sub:sub + 256, :]
            back_two = back[pl.ds(pl.multiple_of(offset + sub, 256), 256), :]
            dh_one = lax.dot_general(back_two, w_out[...], CONTRACT_COLS, preferred_element_type=jnp.float32)
            dz_one = jnp.where(z_one.astype(jnp.float32) > 0, dh_one, 0.0).astype(jnp.bfloat16)
            store_table(table, offset + sub, dz_one.astype(jnp.float32), 2)
    stream_rows([z_hbm], [z_buf], sems, phase * nodes, nodes, z_buf.shape[1], use)


def params():
    return pltpu.CompilerParams(vmem_limit_bytes=VMEM, dimension_semantics=("arbitrary", "arbitrary"))


def forward_specs(weights, last):
    slots = weights.shape[1]
    rows = STEP_SUBS * SUB_ROWS
    w_spec = pl.BlockSpec((1, slots, rows), lambda k, t: (k, 0, t))

    def out_spec(width):
        return pl.BlockSpec((rows, width), lambda k, t: (jnp.where(k == last, t, 0), 0))
    ids = pltpu.SMEM((BUF_SUBS * slots * SUB_ROWS,), jnp.int32)
    return w_spec, out_spec, [ids, ids]


def layer_one(idx, weights, x_all, w_hidden, w_out_pad):
    phases, slots, rows = weights.shape
    nodes, feat = x_all.shape
    hid = w_hidden.shape[1]
    whole = pl.BlockSpec(memory_space=pltpu.VMEM)
    any_spec = pl.BlockSpec(memory_space=pl.ANY)
    w_spec, out_spec, ids = forward_specs(weights, phases - 1)
    stage = pltpu.VMEM((2 * slots * SUB_ROWS, LANES), jnp.float32)
    return pl.pallas_call(
        layer_one_kernel,
        grid=(phases, rows // (STEP_SUBS * SUB_ROWS)),
        in_specs=[any_spec, w_spec, any_spec, whole, whole],
        out_specs=[out_spec(hid), out_spec(LANES)],
        out_shape=[jax.ShapeDtypeStruct((rows, hid), jnp.bfloat16), jax.ShapeDtypeStruct((rows, LANES), jnp.bfloat16)],
        scratch_shapes=[
            pltpu.VMEM((2 * nodes // phases, LANES), jnp.float32), pltpu.VMEM((rows, hid), jnp.float32),
            *ids, stage, stage, pltpu.VMEM((2, 2048, feat), jnp.bfloat16),
            pltpu.SemaphoreType.DMA((1, 2)), pltpu.SemaphoreType.DMA((2,))],
        compiler_params=params(),
        cost_estimate=pl.CostEstimate(flops=2 * 10**11, bytes_accessed=10**8, transcendentals=0),
        name="layer_one")(idx, weights, x_all, w_hidden, w_out_pad)


def layer_two(idx, weights, p_all):
    phases, slots, rows = weights.shape
    any_spec = pl.BlockSpec(memory_space=pl.ANY)
    w_spec, out_spec, ids = forward_specs(weights, phases - 1)
    stage = pltpu.VMEM((slots * SUB_ROWS, LANES), jnp.float32)
    return pl.pallas_call(
        functools.partial(layer_two_kernel, rows),
        grid=(phases, rows // (STEP_SUBS * SUB_ROWS)),
        in_specs=[any_spec, w_spec, any_spec],
        out_specs=out_spec(LANES),
        out_shape=jax.ShapeDtypeStruct((rows, LANES), jnp.float32),
        scratch_shapes=[
            pltpu.VMEM((2 * rows + 128, LANES), jnp.float32), pltpu.VMEM((rows, LANES), jnp.float32),
            *ids, stage, stage, pltpu.VMEM((2, packed_rows(rows) // 6, LANES), jnp.bfloat16),
            pltpu.SemaphoreType.DMA((1, 2)), pltpu.SemaphoreType.DMA((2,))],
        compiler_params=params(),
        cost_estimate=pl.CostEstimate(flops=2 * 10**11, bytes_accessed=10**8, transcendentals=0),
        name="layer_two")(idx, weights, p_all)


def segment_product(name, build, plan, sources, specs, buffers, num_out, width, rows):
    idx, cols, weights, scalars = plan
    phases, edges = cols.shape
    per_step = CHUNK * STEP_CHUNKS
    steps = edges // per_step
    any_spec = pl.BlockSpec(memory_space=pl.ANY)
    tile_spec = pl.BlockSpec((1, 1, per_step), lambda p, t, *_: (p * steps + t, 0, 0))
    ids = pltpu.SMEM((BUF_CHUNKS * CHUNK,), jnp.int32)
    stage = pltpu.VMEM((width * CHUNK, LANES), jnp.float32)
    grid_spec = pltpu.PrefetchScalarGridSpec(
        num_scalar_prefetch=len(scalars),
        grid=(phases, steps),
        in_specs=[any_spec, tile_spec, tile_spec, *specs],
        out_specs=any_spec,
        scratch_shapes=[
            pltpu.VMEM((width * rows + (128 if width == 1 else 0), LANES), jnp.float32),
            pltpu.VMEM((num_out, width * LANES), jnp.float32),
            ids, ids, pltpu.SMEM((per_step,), jnp.int32), stage, stage,
            pltpu.SemaphoreType.DMA((len(buffers), 2)), pltpu.SemaphoreType.DMA((2,)), pltpu.SemaphoreType.DMA, *buffers])
    return pl.pallas_call(
        functools.partial(segment_kernel, width, len(sources), functools.partial(build, rows)),
        grid_spec=grid_spec,
        out_shape=jax.ShapeDtypeStruct((num_out, width * LANES), jnp.float32),
        compiler_params=params(),
        cost_estimate=pl.CostEstimate(flops=2 * 10**11, bytes_accessed=10**8, transcendentals=0),
        name=name)(*scalars, (idx * width).reshape(-1), cols.reshape(phases * steps, 1, per_step),
                   weights.reshape(phases * steps, 1, per_step), *sources)


def sorted_edges(cols_blk, mask_blk, vals_blk, col_blocks, blk_nodes, turn):
    slots = cols_blk.shape[0]
    col_nodes = 2 * blk_nodes
    row_ids = lax.broadcasted_iota(jnp.int32, (slots, col_blocks, blk_nodes), 2)
    valid = mask_blk.reshape(slots, col_blocks, blk_nodes) > 0
    turned = jnp.bitwise_xor(cols_blk, turn).reshape(slots, col_blocks, blk_nodes)
    keys = jnp.where(valid, turned, col_nodes) * blk_nodes + row_ids
    weights = jnp.where(valid, vals_blk.reshape(slots, col_blocks, blk_nodes).astype(jnp.float32), 0.0)
    keys = keys.transpose(1, 0, 2).reshape(col_blocks, slots * blk_nodes)
    weights = weights.transpose(1, 0, 2).reshape(col_blocks, slots * blk_nodes)
    keys, weights = lax.sort((keys, weights), dimension=1, num_keys=1, is_stable=False)
    cols, rows = keys // blk_nodes, keys % blk_nodes
    chunked = cols.reshape(-1, CHUNK)
    base = jnp.minimum(chunked[:, 0] // 8 * 8, col_nodes - WINDOW)
    last = jnp.max(jnp.where(chunked < col_nodes, chunked, -1), axis=1)
    over = jnp.max((last >= base + WINDOW).astype(jnp.int32).reshape(-1, STEP_CHUNKS), axis=1)
    count = jnp.sum(mask_blk.reshape(slots, col_blocks, blk_nodes), axis=(0, 2))
    active = (count + STEP_CHUNKS * CHUNK - 1) // (STEP_CHUNKS * CHUNK)
    return rows, cols, weights, (active, over, base, last)


def solution(mesh):
    row_size = mesh.shape["row"]
    col_size = mesh.shape["col"]
    both_axes = ("row", "col")
    swap = [(0, 1), (1, 0)]

    def device_step(feat_blk, w_hidden, w_output, cols_blk, vals_blk, mask_blk, labels_blk, train_blk):
        row_i, col_j = lax.axis_index("row"), lax.axis_index("col")
        blk_nodes = feat_blk.shape[0]
        col_nodes = blk_nodes * row_size
        packed = packed_rows(blk_nodes)
        slots = cols_blk.shape[0]
        classes = w_output.shape[1]
        any_spec = pl.BlockSpec(memory_space=pl.ANY)
        whole = pl.BlockSpec(memory_space=pltpu.VMEM)
        w_out_pad = jnp.pad(w_output, ((0, 0), (0, LANES - classes)))

        x_all = lax.all_gather(feat_blk, both_axes, axis=0, tiled=True)
        own_cols = lax.all_to_all(cols_blk, "col", split_axis=1, concat_axis=0, tiled=True)
        own_w = lax.all_to_all(vals_blk * mask_blk.astype(jnp.bfloat16), "col", split_axis=1, concat_axis=0, tiled=True)
        own_w = own_w.astype(jnp.float32).reshape(col_size, slots, blk_nodes)
        own_cols = own_cols.reshape(col_size, slots, -1, STEP_SUBS, SUB_ROWS).transpose(0, 2, 3, 1, 4).reshape(-1)
        train_count = jnp.maximum(lax.psum(jnp.sum(train_blk), both_axes), 1).astype(jnp.float32)

        plan = sorted_edges(cols_blk, mask_blk, vals_blk, col_size, blk_nodes, (1 - row_i) * blk_nodes)
        x_all, plan, train_count = lax.optimization_barrier((x_all, plan, train_count))

        z_one, proj_two = layer_one(own_cols * 2, own_w, x_all, w_hidden, w_out_pad)
        p_all = lax.all_gather(pack_nodes(proj_two[:, :classes]), both_axes, axis=0, tiled=True)
        z_one, p_all = lax.optimization_barrier((z_one, p_all))
        z_all = lax.all_gather(z_one, "col", axis=0, tiled=True)
        z_two = layer_two(own_cols, own_w, p_all)[:, :classes]

        mask_f = train_blk.astype(jnp.float32)
        log_norm = jax.nn.logsumexp(z_two, axis=1)
        onehot = (labels_blk[:, None] == jnp.arange(classes, dtype=jnp.int32)[None, :]).astype(jnp.float32)
        picked = jnp.sum(z_two * onehot, axis=1)
        loss_mean = jnp.sum(mask_f * (log_norm - picked)) / train_count
        softmax_z = jnp.exp(z_two - log_norm[:, None])
        grad_two = ((mask_f / train_count)[:, None] * (softmax_z - onehot)).astype(jnp.bfloat16)
        z_all, grad_two = lax.optimization_barrier((z_all, grad_two))
        grad_rows = lax.all_gather(pack_nodes(grad_two), "col", axis=0, tiled=True)

        row_buf = pltpu.VMEM((2, packed // 6, LANES), jnp.bfloat16)
        part_two = segment_product(
            "back_two", build_packed, plan, [grad_rows], [any_spec], [row_buf], col_nodes, 1, blk_nodes)
        other = lax.ppermute(part_two[:blk_nodes], "row", swap)
        back_two = (part_two[blk_nodes:] + other).astype(jnp.bfloat16)
        back_all = lax.all_gather(pack_nodes(back_two[:, :classes]), ("col", "row"), axis=0, tiled=True)
        back_rows = lax.dynamic_slice_in_dim(back_all, row_i * col_size * packed, col_size * packed, 0)
        back_own = lax.dynamic_slice_in_dim(back_rows, col_j * packed, packed, 0)
        back_own = jnp.concatenate([back_own[:, q * pack_lanes():q * pack_lanes() + classes] for q in range(PACK)], axis=0)[:blk_nodes]
        h_one = jnp.maximum(z_one, 0)
        grad_w_output = lax.dot_general(h_one, back_own, CONTRACT_ROWS, preferred_element_type=jnp.float32)

        part_one = segment_product(
            "back_one", build_dz, plan, [z_all, back_rows, w_out_pad], [any_spec, any_spec, whole],
            [pltpu.VMEM((2, 1024, 2 * LANES), jnp.bfloat16), row_buf,
             pltpu.VMEM((blk_nodes + 128, LANES), jnp.bfloat16)],
            col_nodes, 2, blk_nodes)
        other = lax.ppermute(part_one[:blk_nodes], "row", swap)
        back_one = (part_one[blk_nodes:] + other).astype(jnp.bfloat16)
        feat_src = lax.dynamic_slice_in_dim(x_all, (col_j * row_size + row_i) * blk_nodes, blk_nodes, 0)
        grad_w_hidden = lax.dot_general(feat_src, back_one, CONTRACT_ROWS, preferred_element_type=jnp.float32)
        loss_mean, grad_w_hidden, grad_w_output = lax.psum((loss_mean, grad_w_hidden, grad_w_output), both_axes)
        return loss_mean, grad_w_hidden, grad_w_output

    node_spec = P(("row", "col"), None)
    label_spec = P(("row", "col"))
    adj_spec = P("col", "row")
    return jax.shard_map(device_step, mesh=mesh, in_specs=(node_spec, P(), P(), adj_spec, adj_spec, adj_spec, label_spec, label_spec), out_specs=(P(), P(), P()), check_vma=False)
```

time: 3260 us -> 1750 us (0.54)
  Pallas kernels: 2100 us -> 1080 us
  waiting for transfers between devices: 769 us -> 260 us
    pallas_call x4, Pallas kernels: 2100 us -> 1080 us  [the longest x2 562 us: segment_product(): pl.pallas_call(functools.partial(segment_kernel, width, len(sources), fun...]
    all_gather x1, waiting for transfers between devices: 279 us -> 35.1 us  [device_step(): z_all = lax.all_gather(z_one, 'col', axis=0, tiled=True)]
    all_gather x1, waiting for transfers between devices: 123 us -> 0.01 us  [device_step(): x_all = lax.all_gather(feat_blk, both_axes, axis=0, tiled=True)]
    all_gather x3, waiting for transfers between devices: 285 us -> 173 us  [the longest x1 60.7 us: device_step(): lax.all_gather(pack_nodes(proj_two[:, :classes]), both_axes, axis=0, tile...]
  transfers between devices with their start and end apart: 10 -> 10, of which waited for: 9 -> 8; matrix products, arithmetic and copies ran while one was open for 7% -> 15% of each run, Pallas kernels for 0% -> 13%
where the time goes in v2:
time: 1750 us; the launch traced here: 1730 us
  Pallas kernels  1080 us (62%)
  waiting for transfers between devices  260 us (15%)
  other arithmetic  238 us (14%)
  local copies, waits for them, and re-layouts  57 us (3%)
  blocking collectives  51 us (3%)
  matrix products  18.9 us (1%)
    pallas_call x2, Pallas kernels, segment_product(): pl.pallas_call(functools.partial(segment_kernel, width, len(sources), fun...  562 us
    pallas_call x1, Pallas kernels, layer_one(): pl.pallas_call(layer_one_kernel, grid=(phases, rows // (STEP_SUBS * SUB_R...  284 us
    pallas_call x1, Pallas kernels, layer_two(): pl.pallas_call(functools.partial(layer_two_kernel, rows), grid=(phases, r...  233 us
    sort x1, other arithmetic, sorted_edges(): lax.sort((keys, weights), dimension=1, num_keys=1, is_stable=False)  191 us
    all_gather x1, waiting for transfers between devices, device_step(): lax.all_gather(pack_nodes(proj_two[:, :classes]), both_axes, axis=0, tile...  60.7 us
    all_gather x1, waiting for transfers between devices, device_step(): lax.all_gather(pack_nodes(back_two[:, :classes]), ('col', 'row'), axis=0,...  60.4 us
    all_gather x1, waiting for transfers between devices, device_step(): grad_rows = lax.all_gather(pack_nodes(grad_two), 'col', axis=0, tiled=True)  52.3 us
    all_gather x1, waiting for transfers between devices, device_step(): z_all = lax.all_gather(z_one, 'col', axis=0, tiled=True)  35.1 us
  transfers between devices with their start and end apart: 10, of which 8 were waited for; matrix products, arithmetic and copies ran while one was open for 15% of the time, Pallas kernels for 13%

profile of v2, /device:TPU:0, one launch (start us, length us, event | category | flops | bytes accessed | tf_op | source)
XLA Modules:
  0.0 1729.4 jit_solution(5931434359818832606)
XLA Ops:
  7.2 0.7 all-gather.6.cloned.1.call-update
  8.6 1.1 convert_multiply_fusion
  9.7 0.6 reduce_sum.55
  10.3 5.6 all-to-all-start.1
  15.9 26.7 %psum.28 = s32[]{:T(128)} all-reduce(s32[]{:T(128)} %reduce_sum.55), channel_id=1, replica_groups=mesh['col'=4,'row'=2] {'row','col'}, use_global_device_ids=true, to_apply=%region_6.7 | all-reduce | flops 1 | bytes 8 | tf_op jit(solution)/shard_map/psum | solution.py:452
  42.5 0.6 reduce_sum.52
  43.2 0.5 convert_select_fusion
  43.7 1.7 select_multiply_fusion
  45.4 0.9 mul.67
  46.3 0.9 select_n.66
  47.8 190.6 %sort.15 = (s32[4,65536]{1,0:T(4,128)S(1)}, f32[4,65536]{1,0:T(4,128)}) sort(s32[4,65536]{1,0:T(4,128)S(1)} %bitcast.29, f32[4,65536]{1,0:T(4,128)S(1)} %bitcast.28), dimensions={1}, to_apply=%region_0.1 | sort | flops 4718592 | bytes 4194304 | tf_op jit(solution)/shard_map/sort | solution.py:419
  238.3 2.8 add_select_fusion
  241.1 0.7 reshape.77
  242.1 0.5 copy-done.14
  244.0 0.7 pad.24.w_output.refs_2_
  244.7 0.6 convert_reduce_fusion.over_ref
  245.3 0.6 and_select_fusion.active_ref
  245.8 0.6 fusion.33.base_ref
  246.5 3.7 all-to-all-start
  250.2 2.1 convert_bitcast_fusion.w_ref
  252.3 11.5 all-to-all-done
  263.8 0.9 reshape.73
  264.7 0.7 copy.33
  265.4 0.5 copy.46
  265.9 1.0 copy-done.7
  266.9 1.1 broadcast_multiply_fusion.idx_hbm
  268.0 283.9 %layer_one.1 = (bf16[16384,256]{1,0:T(8,128)(2,1)}, bf16[16384,128]{1,0:T(8,128)(2,1)}) custom-call(s32[262144]{0:T(1024)} %broadcast_multiply_fusion.idx_hbm, f32[4,4,16384]{2,1,0:T(4,128)} %convert_bitcast_fusion.w_ref, bf16[131072,128]{1,0:T(8,128)(2,1)} %all-gather.6.cloned.1.call-done.x_hbm, bf16[128,256]{1,0:T(8,128)(2,1)} %w_hidden.1, ...), custom_call_target="tpu_custom_call" | custom-call | flops 199999995904 | bytes 100000000 | tf_op jit(solution)/shard_map/layer_one/pallas_call | solution.py:345
  551.9 2.6 fusion.41
  554.4 2.6 fusion.18
  557.1 60.7 %all-gather.8.cloned.1.call-done.p_hbm = bf16[43776,128]{1,0:T(8,128)(2,1)} async-done(((bf16[5472,128]{1,0:T(8,128)(2,1)}), bf16[43776,128]{1,0:T(8,128)(2,1)}) %all-gather.8.cloned.1.call-update) | async-done | bytes 11206672 | tf_op jit(solution)/shard_map/all_gather | solution.py:458
  617.9 233.0 %layer_two.1 = f32[16384,128]{1,0:T(8,128)} custom-call(s32[262144]{0:T(1024)} %bitcast.26, f32[4,4,16384]{2,1,0:T(4,128)} %convert_bitcast_fusion.w_ref, bf16[43776,128]{1,0:T(8,128)(2,1)} %all-gather.8.cloned.1.call-done.p_hbm), custom_call_target="tpu_custom_call" | custom-call | flops 199999995904 | bytes 100000000 | tf_op jit(solution)/shard_map/layer_two/pallas_call | solution.py:365
  851.0 5.7 slice_reduce_fusion
  856.8 10.2 select_reduce_fusion
  867.0 0.6 multiply_reduce_fusion
  867.6 8.5 multiply_convert_fusion
  876.2 35.1 %all-gather.10.cloned.1.call-done.refs_0_ = bf16[65536,256]{1,0:T(8,128)(2,1)} async-done(((bf16[16384,256]{1,0:T(8,128)(2,1)}), bf16[65536,256]{1,0:T(8,128)(2,1)}) %all-gather.10.cloned.1.call-update) | async-done | bytes 33554448 | tf_op jit(solution)/shard_map/all_gather | solution.py:460
  911.3 2.6 fusion.40
  913.9 2.7 fusion.22
  916.6 1.0 copy.48
  917.6 0.5 copy-done.5
  918.1 2.4 reshape.79.col_ref
  920.5 2.4 reshape.80.w_ref
  922.9 52.3 %all-gather.12.cloned.1.call-done.refs_0_ = bf16[21888,128]{1,0:T(8,128)(2,1)} async-done(((bf16[5472,128]{1,0:T(8,128)(2,1)}), bf16[21888,128]{1,0:T(8,128)(2,1)}) %all-gather.12.cloned.1.call-update) | async-done | bytes 5603344 | tf_op jit(solution)/shard_map/all_gather | solution.py:471
  975.3 239.9 %back_two.1 = f32[32768,128]{1,0:T(8,128)} custom-call(s32[4]{0:T(128)} %and_select_fusion.active_ref, s32[128]{0:T(128)} %convert_reduce_fusion.over_ref, s32[1024]{0:T(1024)} %fusion.33.base_ref, s32[1024]{0:T(1024)} %copy-done.14, s32[262144]{0:T(1024)} %bitcast.33, s32[128,1,2048]{2,1,0:T(1,128)} %reshape.79.col_ref, f32[128,1,2048]{2,1,0:T(1,128)} %reshape.80.w_ref, ...), custom_call_target="tpu_custom_call" | custom-call | flops 199999995904 | bytes 100000000 | tf_op jit(solution)/shard_map/back_two/pallas_call | solution.py:399
  1215.2 3.9 slice.97
  1219.1 13.1 collective-permute-done
  1232.3 0.8 fusion.3
  1233.6 2.7 fusion.20
  1236.6 1.1 copy.47
  1237.7 60.4 %all-gather.14.cloned.1.call-done = bf16[43776,128]{1,0:T(8,128)(2,1)} async-done(((bf16[5472,128]{1,0:T(8,128)(2,1)}), bf16[43776,128]{1,0:T(8,128)(2,1)}) %all-gather.14.cloned.1.call-update) | async-done | bytes 11206672 | tf_op jit(solution)/shard_map/all_gather | solution.py:478
  1298.0 6.0 constant_dynamic-slice_fusion.1.refs_1_
  1304.1 322.4 %back_one.1 = f32[32768,256]{1,0:T(8,128)} custom-call(s32[4]{0:T(128)} %and_select_fusion.active_ref, s32[128]{0:T(128)} %convert_reduce_fusion.over_ref, s32[1024]{0:T(1024)} %fusion.33.base_ref, s32[1024]{0:T(1024)} %copy-done.14, s32[262144]{0:T(1024)} %bitcast.32, s32[128,1,2048]{2,1,0:T(1,128)} %reshape.79.col_ref, f32[128,1,2048]{2,1,0:T(1,128)} %reshape.80.w_ref, ...), custom_call_target="tpu_custom_call" | custom-call | flops 199999995904 | bytes 100000000 | tf_op jit(solution)/shard_map/back_one/pallas_call | solution.py:399
  1626.4 11.3 slice.102
  1638.4 4.9 fusion.38
  1643.3 1.8 copy.41
  1645.1 1.7 copy.42
  1646.8 1.2 copy.43
  1648.0 3.2 concatenate.15
  1651.2 11.6 collective-permute-done.1
  1662.8 14.3 fusion.1
  1677.1 4.6 fusion.4
  1681.7 24.4 %all-reduce.7 = (f32[]{:T(128)}, f32[256,40]{0,1:T(8,128)}) all-reduce(f32[]{:T(128)S(6)} %div.69, f32[256,40]{0,1:T(8,128)S(1)} %fusion.4), channel_id=1, replica_groups=mesh['col'=4,'row'=2] {'row','col'}, use_global_device_ids=true, to_apply=%region_11.12 | all-reduce | flops 10241 | bytes 81928 | tf_op jit(solution)/shard_map/psum | solution.py:494
  1706.1 14.5 all-reduce.10.cloned.1.call-done
  1720.6 1.6 copy.50
  (57 shorter events, 3.4 us)
Async XLA Ops:
  7.2 1.0 copy-start.8
  7.2 1.4 copy-start.6
  7.2 2.5 copy-start.11
  7.2 260.8 %all-gather.6.cloned.1.call-start = ((), (), s32[]{:S(2)}) async-start(), calls=%async_computation.2 | async-start | bytes 37748736 | tf_op jit(solution)/shard_map/all_gather | solution.py:447
  10.3 236.1 %all-to-all-start.1 = ((bf16[4,4,16384]{2,0,1:T(4,128)(2,1)}), bf16[4,4,16384]{2,0,1:T(4,128)(2,1)}, u32[]{:S(2)}, u32[]{:S(2)}) async-start(bf16[4,4,16384]{2,0,1:T(4,128)(2,1)} %bitcast.3), calls=%async_computation.1 | async-start | bytes 1048576 | tf_op jit(solution)/shard_map/all_to_all | solution.py:449
  241.1 5.4 copy-start.4
  241.1 2.8 copy-start.13
  242.0 0.6 copy-start.14
  246.5 17.3 %all-to-all-start = ((s32[4,4,16384]{2,0,1:T(4,128)}), s32[4,4,16384]{2,0,1:T(4,128)S(1)}, u32[]{:S(2)}, u32[]{:S(2)}) async-start(s32[4,4,16384]{2,0,1:T(4,128)} %bitcast), calls=%async_computation | async-start | bytes 2097152 | tf_op jit(solution)/shard_map/all_to_all | solution.py:448
  250.2 367.7 %all-gather.8.cloned.1.call-start = ((), (), s32[]{:S(2)}) async-start(), calls=%async_computation.3 | async-start | bytes 12607488 | tf_op jit(solution)/shard_map/all_gather | solution.py:458
  265.9 1.0 copy-start.7
  557.1 354.2 %all-gather.10.cloned.1.call-start = ((), (), s32[]{:S(2)}) async-start(), calls=%async_computation.4 | async-start | bytes 41943040 | tf_op jit(solution)/shard_map/all_gather | solution.py:460
  617.9 357.4 %all-gather.12.cloned.1.call-start = ((), (), s32[]{:S(2)}) async-start(), calls=%async_computation.5 | async-start | bytes 7004160 | tf_op jit(solution)/shard_map/all_gather | solution.py:471
  850.9 5.8 copy-start
  850.9 5.8 copy-start.10
  856.8 10.2 copy-start.12
  913.8 2.7 copy-start.2
  916.5 1.6 copy-start.5
  916.5 4.0 copy-start.9
  916.5 381.5 %all-gather.14.cloned.1.call-start = ((), (), s32[]{:S(2)}) async-start(), calls=%async_computation.6 | async-start | bytes 12607488 | tf_op jit(solution)/shard_map/all_gather | solution.py:478
  1215.2 17.1 copy-start.1
  1219.1 13.2 collective-permute-start
  1233.6 2.7 copy-start.3
  1236.3 484.3 %all-reduce.10.cloned.1.call-start = ((), (), s32[]{:S(2)}) async-start(), calls=%async_computation.7 | async-start | bytes 262144 | tf_op jit(solution)/shard_map/psum | solution.py:494
  1637.7 25.1 %collective-permute-start.1 = (f32[16384,256]{1,0:T(8,128)}, f32[16384,256]{1,0:T(8,128)}, u32[]{:S(2)}, u32[]{:S(2)}) collective-permute-start(f32[16384,256]{1,0:T(8,128)} %slice.102), channel_id=1, source_target_pairs={{0,1},{1,0},{2,3},{3,2},{4,5},{5,4},{6,7},{7,6}} | collective-permute-start | bytes 50331656 | tf_op jit(solution)/shard_map/ppermute | solution.py:490
Sparse Core Ops, SparseCore 0:
  9.8 159.1 all-gather.5
  557.2 60.6 all-gather.7
  619.7 291.5 all-gather.9
  916.7 58.5 all-gather.11
  1236.4 61.5 all-gather.13
  1677.3 43.2 all-reduce.9

commit v3 on v2

v3 whole, which is shorter than its diff:
```python
import functools

import jax
import jax.numpy as jnp
from jax import lax
from jax.experimental import pallas as pl
from jax.experimental.pallas import tpu as pltpu
from jax.sharding import PartitionSpec as P


CONTRACT_ROWS = (((0,), (0,)), ((), ()))
CONTRACT_COLS = (((1,), (1,)), ((), ()))
LANES = 128
SUB_ROWS = 256
STEP_SUBS = 4
PIECE_ROWS = 32
PIECES = 8
BUF_SUBS = 1
CHUNK = 256
BUF_CHUNKS = 2
STEP_CHUNKS = 16
WINDOW = 256
PACK = 3
INNER = 4
VMEM = 63 << 20


def copy_row(ids, e, table, stage, at, width):
    if width == 1:
        stage[at, :] = table[ids[e], :]
    else:
        stage[width * at:width * (at + 1), :] = table[pl.ds(pl.multiple_of(ids[e], width), width), :]


def index_copy(idx_hbm, ids, sems, buf, step):
    size = ids[buf].shape[0]
    start = pl.multiple_of((step * len(ids) + buf) * size, size)
    return pltpu.make_async_copy(idx_hbm.at[pl.ds(start, size)], ids[buf], sems.at[buf])


def start_next(idx_hbm, ids, sems, buf, following, total):
    @pl.when(following < total)
    def _():
        index_copy(idx_hbm, ids, sems, buf, following).start()


def store_table(table, first, value, width):
    rows = value.shape[0]
    for part in range(width):
        piece = value[:, part * LANES:(part + 1) * LANES]
        if width == 1:
            table[pl.ds(pl.multiple_of(first, rows), rows), :] = piece
        else:
            table[pl.ds(width * first + part, rows, stride=width), :] = piece


def stream_rows(source, buffer, sems, phase, phases, total, use):
    slots, chunk = buffer.shape[0], buffer.shape[1]
    steps = total // chunk
    assert steps % slots == 0

    def copy(step, slot):
        start = pl.multiple_of(phase * total + step * chunk, 16)
        return pltpu.make_async_copy(source.at[pl.ds(start, chunk), :], buffer.at[slot], sems.at[slot])

    @pl.when(phase == 0)
    def _():
        for slot in range(slots):
            copy(slot, slot).start()

    def body(group, carry):
        for slot in range(slots):
            step = group * slots + slot
            copy(step, slot).wait()
            use(buffer.at[slot], step * chunk)

            @pl.when((step + slots < steps) | (phase + 1 < phases))
            def _():
                copy(step + slots, slot).start()
        return carry

    lax.fori_loop(0, steps // slots, body, 0)


def weight_columns(w_ref, first):
    w_rows = w_ref[0, :, pl.ds(pl.multiple_of(first, LANES), LANES)]
    return jnp.concatenate([w_rows] * (8 // w_ref.shape[1]), axis=0).T


def weighted_sum(stage, w_cols, slots, first, size, width):
    parts = [None] * width
    inside = first % LANES
    for slot in range(slots):
        column = jnp.broadcast_to(w_cols[inside:inside + size, slot:slot + 1], (size, LANES))
        at = width * (slot * SUB_ROWS + first)
        for part in range(width):
            rows = stage[pl.ds(at + part, size, stride=width), :] if width > 1 else stage[at:at + size, :]
            term = column * rows
            parts[part] = term if slot == 0 else parts[part] + term
    return parts


def forward_step(idx_hbm, w_ref, table, acc, ids, stages, idx_sems, width):
    phase, tile = pl.program_id(0), pl.program_id(1)
    per_phase = pl.num_programs(1) * INNER
    total = pl.num_programs(0) * per_phase
    slots = w_ref.shape[1]
    edges = slots * SUB_ROWS
    pieces = SUB_ROWS // PIECE_ROWS
    step_rows = STEP_SUBS * SUB_ROWS

    @pl.when((phase == 0) & (tile == 0))
    def _():
        for buf in range(len(ids)):
            index_copy(idx_hbm, ids, idx_sems, buf, 0).start()

    def inner(n, carry):
        step = phase * per_phase + tile * INNER + n
        first_row = pl.multiple_of((tile * INNER + n) * step_rows, step_rows)

        @pl.when(phase == 0)
        def _():
            acc[pl.ds(first_row, step_rows), :] = jnp.zeros((step_rows, acc.shape[1]), jnp.float32)

        for sub in range(STEP_SUBS + 1):
            buf, part = sub // BUF_SUBS, sub % BUF_SUBS
            if part == 0 and sub < STEP_SUBS:
                index_copy(idx_hbm, ids, idx_sems, buf, step).wait()
            for piece in range(pieces):
                first = piece * PIECE_ROWS
                if sub > 0 and first % LANES == 0:
                    w_cols = weight_columns(w_ref, n * step_rows + (sub - 1) * SUB_ROWS + first)
                if sub < STEP_SUBS:
                    for e in range(piece * edges // pieces, (piece + 1) * edges // pieces):
                        copy_row(ids[buf], part * edges + e, table, stages[sub % len(stages)], e, width)
                if sub > 0:
                    parts = weighted_sum(stages[(sub - 1) % len(stages)], w_cols, slots, first, PIECE_ROWS, width)
                    rows = pl.ds(pl.multiple_of(first_row + (sub - 1) * SUB_ROWS + first, PIECE_ROWS), PIECE_ROWS)
                    for lane in range(width):
                        acc[rows, lane * LANES:(lane + 1) * LANES] += parts[lane]
            if part == BUF_SUBS - 1 and sub < STEP_SUBS:
                start_next(idx_hbm, ids, idx_sems, buf, step + 1, total)
        return carry

    lax.fori_loop(0, INNER, inner, 0)


def finish_rows(acc, use):
    tile = pl.program_id(1)
    size = INNER * STEP_SUBS * SUB_ROWS

    def body(n, carry):
        at = pl.multiple_of(n * 256, 256)
        use(pl.ds(at, 256), acc[pl.ds(pl.multiple_of(tile * size + at, 256), 256), :])
        return carry

    lax.fori_loop(0, size // 256, body, 0)


def layer_one_kernel(idx_hbm, w_ref, x_hbm, w_hidden, w_output, z_ref, p_ref, table, acc, ids_a, ids_b, ids_c, ids_d, stage_a, stage_b, x_buf,
                     sems, idx_sems):
    phase, tile = pl.program_id(0), pl.program_id(1)
    col_nodes = table.shape[0] // 2

    @pl.when(tile == 0)
    def _():
        def use(buf, offset):
            def body(n, carry):
                for part in range(2):
                    sub = pl.multiple_of(n * 512 + part * 256, 256)
                    proj = jnp.dot(buf[pl.ds(sub, 256), :], w_hidden[...], preferred_element_type=jnp.float32)
                    proj = proj.astype(jnp.bfloat16).astype(jnp.float32)
                    store_table(table, offset + sub, proj, 2)
                return carry

            lax.fori_loop(0, x_buf.shape[1] // 512, body, 0)

        stream_rows(x_hbm, x_buf, sems, phase, pl.num_programs(0), col_nodes, use)

    forward_step(idx_hbm, w_ref, table, acc, [ids_a, ids_b, ids_c, ids_d], [stage_a, stage_b], idx_sems, 2)

    @pl.when(phase == pl.num_programs(0) - 1)
    def _():
        def use(at, sums):
            z_one = sums.astype(jnp.bfloat16)
            z_ref[at, :] = z_one
            h_one = jnp.maximum(z_one, 0)
            p_ref[at, :] = jnp.dot(h_one, w_output[...], preferred_element_type=jnp.float32).astype(jnp.bfloat16)

        finish_rows(acc, use)


def unpack_table(table, p_hbm, p_buf, sems, phase, phases, blocks, nodes):
    packed = packed_rows(nodes)
    piece = packed // 18

    def use(buf, offset):
        block = offset // packed

        def body(n, carry):
            inside = pl.multiple_of(n * piece, 16)
            value = buf[pl.ds(inside, piece), :].astype(jnp.float32)
            for q in range(PACK):
                turned = value if q == 0 else pltpu.roll(value, LANES - q * pack_lanes(), 1)
                first = pl.multiple_of(block * nodes + q * packed + inside, 16)
                table[pl.ds(first, piece), :] = turned.astype(table.dtype)
            return carry

        lax.fori_loop(0, 18, body, 0)

    stream_rows(p_hbm, p_buf, sems, phase, phases, blocks * packed, use)


def pack_lanes():
    return LANES // PACK // 8 * 8


def packed_rows(nodes):
    return -(-nodes // (PACK * 96)) * 96


def pack_nodes(values):
    nodes = values.shape[0]
    packed = packed_rows(nodes)
    values = jnp.pad(values, ((0, PACK * packed - nodes), (0, pack_lanes() - values.shape[1])))
    parts = [values[q * packed:(q + 1) * packed] for q in range(PACK)]
    return jnp.pad(jnp.concatenate(parts, axis=1), ((0, 0), (0, LANES - PACK * pack_lanes())))


def layer_two_kernel(nodes, idx_hbm, w_ref, p_hbm, z_ref, table, acc, ids_a, ids_b, ids_c, ids_d, stage_a, stage_b, p_buf, sems, idx_sems):
    phase, tile = pl.program_id(0), pl.program_id(1)

    @pl.when(tile == 0)
    def _():
        unpack_table(table, p_hbm, p_buf, sems, phase, pl.num_programs(0), 2, nodes)

    forward_step(idx_hbm, w_ref, table, acc, [ids_a, ids_b, ids_c, ids_d], [stage_a, stage_b], idx_sems, 1)

    @pl.when(phase == pl.num_programs(0) - 1)
    def _():
        def use(at, sums):
            z_ref[at, :] = sums

        finish_rows(acc, use)


def segment_kernel(width, n_src, build, active_ref, over_ref, base_ref, last_ref, idx_hbm, col_ref, w_ref, *refs):
    bufs = STEP_CHUNKS // BUF_CHUNKS
    sources, refs = refs[:n_src], refs[n_src:]
    (out_first, out_second, table, acc, spare_ids, stage_a, stage_b, idx_sems, spare_sem, out_sems), refs = refs[:10], refs[10:]
    ids, refs = refs[:bufs], refs[bufs:]
    buffers, sems = refs[0::2], refs[1::2]
    stages = [stage_a, stage_b]
    phase, tile = pl.program_id(0), pl.program_id(1)
    steps = pl.num_programs(1) * INNER
    total = pl.num_programs(0) * steps

    @pl.when((phase == 0) & (tile == 0))
    def _():
        for buf in range(len(ids)):
            index_copy(idx_hbm, ids, idx_sems, buf, 0).start()

        def zero(n, carry):
            acc[pl.ds(pl.multiple_of(n * 256, 256), 256), :] = jnp.zeros((256, acc.shape[1]), jnp.float32)
            return carry

        lax.fori_loop(0, acc.shape[0] // 256, zero, 0)

    @pl.when(tile == 0)
    def _():
        build(sources, buffers, sems, phase, pl.num_programs(0), table)

    def gathered(stage):
        lanes = []
        for part in range(width):
            rows = stage[pl.ds(part, CHUNK, stride=width), :] if width > 1 else stage[...]
            lanes.append(rows.astype(jnp.bfloat16))
        return jnp.concatenate(lanes, axis=1) if width > 1 else lanes[0]

    def product(cols, weights, rows, base):
        local = lax.broadcasted_iota(jnp.int32, (WINDOW, CHUNK), 0)
        select = jnp.where(local == cols - base, weights, 0.0).astype(jnp.bfloat16)
        acc[pl.ds(pl.multiple_of(base, 8), WINDOW), :] += jnp.dot(select, rows, preferred_element_type=jnp.float32)

    def inner(n, carry):
        place = tile * INNER + n
        step = phase * steps + place
        following = jnp.where(place + 1 < active_ref[phase], step + 1, (phase + 1) * steps)

        def lanes_of(chunk):
            return pl.ds(pl.multiple_of((n * STEP_CHUNKS + chunk) * CHUNK, CHUNK), CHUNK)

        def multiply(chunk):
            part = lanes_of(chunk)
            base = base_ref[step * STEP_CHUNKS + chunk]
            local = lax.broadcasted_iota(jnp.int32, (WINDOW, CHUNK), 0)
            select = jnp.where(local == col_ref[0, :, part] - base, w_ref[0, :, part], 0.0).astype(jnp.bfloat16)
            return base, jnp.dot(select, gathered(stages[chunk % 2]), preferred_element_type=jnp.float32)

        size = WINDOW // PIECES
        for chunk in range(STEP_CHUNKS + 1):
            buf, part = chunk // BUF_CHUNKS, chunk % BUF_CHUNKS
            if part == 0 and chunk < STEP_CHUNKS:
                index_copy(idx_hbm, ids, idx_sems, buf, step).wait()
            if chunk > 0:
                base, sums = multiply(chunk - 1)
            for piece in range(PIECES):
                if chunk < STEP_CHUNKS:
                    for e in range(piece * CHUNK // PIECES, (piece + 1) * CHUNK // PIECES):
                        copy_row(ids[buf], part * CHUNK + e, table, stages[chunk % 2], e, width)
                if chunk > 0:
                    at = pl.ds(pl.multiple_of(base + piece * size, 8), size)
                    acc[at, :] += sums[piece * size:(piece + 1) * size, :]
            if part == BUF_CHUNKS - 1 and chunk < STEP_CHUNKS:
                start_next(idx_hbm, ids, idx_sems, buf, following, total)

        @pl.when(over_ref[step] > 0)
        def _():
            wide_chunks(n, step)

        return carry

    def wide_chunks(n, step):
        size = STEP_CHUNKS * CHUNK
        copy = pltpu.make_async_copy(idx_hbm.at[pl.ds(pl.multiple_of(step * size, size), size)], spare_ids, spare_sem)
        copy.start()
        copy.wait()

        def wide(chunk, carry):
            base, last = base_ref[step * STEP_CHUNKS + chunk], last_ref[step * STEP_CHUNKS + chunk]

            @pl.when(last >= base + WINDOW)
            def _():
                def fetch(e, carry):
                    copy_row(spare_ids, chunk * CHUNK + e, table, stage_a, 0, width)
                    if width == 1:
                        stage_b[pl.ds(e, 1), :] = stage_a[0:1, :]
                    else:
                        stage_b[pl.ds(width * e, width), :] = stage_a[0:width, :]
                    return carry

                lax.fori_loop(0, CHUNK, fetch, 0)
                part = pl.ds(pl.multiple_of((n * STEP_CHUNKS + chunk) * CHUNK, CHUNK), CHUNK)
                cols, weights = col_ref[0, :, part], w_ref[0, :, part]
                rows = gathered(stage_b)
                end = acc.shape[0] - WINDOW

                def more(window, carry):
                    start = base + window * WINDOW
                    fresh = jnp.where(cols >= start, weights, 0.0)
                    product(cols, fresh, rows, jnp.minimum(start, end))
                    return carry

                lax.fori_loop(1, (last - base) // WINDOW + 1, more, 0)

            return carry

        lax.fori_loop(0, STEP_CHUNKS, wide, 0)

    lax.fori_loop(0, jnp.clip(active_ref[phase] - tile * INNER, 0, INNER), inner, 0)

    @pl.when((phase == pl.num_programs(0) - 1) & (tile == pl.num_programs(1) - 1))
    def _():
        half = acc.shape[0] // 2
        copies = [pltpu.make_async_copy(acc.at[pl.ds(n * half, half), :], out, out_sems.at[n])
                  for n, out in enumerate([out_first, out_second])]
        for copy in copies:
            copy.start()
        for copy in copies:
            copy.wait()


def build_packed(nodes, sources, buffers, sems, phase, phases, table):
    unpack_table(table, sources[0], buffers[0], sems[0], phase, phases, 1, nodes)


def build_dz(nodes, sources, buffers, sems, phase, phases, table):
    z_first, z_second, b_hbm, w_out = sources
    z_buf, b_buf, back = buffers
    half = nodes // 2
    unpack_table(back, b_hbm, b_buf, sems[1], phase, phases, 1, nodes)

    def use(buf, offset):
        for sub in range(0, z_buf.shape[2], 256):
            z_one = buf[sub:sub + 256, :]
            back_two = back[pl.ds(pl.multiple_of(offset + sub, 256), 256), :]
            dh_one = lax.dot_general(back_two, w_out[...], CONTRACT_COLS, preferred_element_type=jnp.float32)
            dz_one = jnp.where(z_one.astype(jnp.float32) > 0, dh_one, 0.0).astype(jnp.bfloat16)
            store_table(table, offset + sub, dz_one.astype(jnp.float32), 2)

    stream_rows(z_first, z_buf.at[0], sems[0].at[0], phase, phases, half, use)
    stream_rows(z_second, z_buf.at[1], sems[0].at[1], phase, phases, half, lambda buf, offset: use(buf, half + offset))


def params():
    return pltpu.CompilerParams(vmem_limit_bytes=VMEM, dimension_semantics=("arbitrary", "arbitrary"))


def forward_specs(weights, last):
    slots = weights.shape[1]
    rows = INNER * STEP_SUBS * SUB_ROWS
    w_spec = pl.BlockSpec((1, slots, rows), lambda k, t: (k, 0, t))

    def out_spec(width):
        return pl.BlockSpec((rows, width), lambda k, t: (jnp.where(k == last, t, 0), 0))

    ids = pltpu.SMEM((BUF_SUBS * slots * SUB_ROWS,), jnp.int32)
    return w_spec, out_spec, [ids] * (STEP_SUBS // BUF_SUBS)


def layer_one(idx, weights, x_all, w_hidden, w_out_pad):
    phases, slots, rows = weights.shape
    nodes, feat = x_all.shape
    hid = w_hidden.shape[1]
    whole = pl.BlockSpec(memory_space=pltpu.VMEM)
    any_spec = pl.BlockSpec(memory_space=pl.ANY)
    w_spec, out_spec, ids = forward_specs(weights, phases - 1)
    stage = pltpu.VMEM((2 * slots * SUB_ROWS, LANES), jnp.float32)
    return pl.pallas_call(
        layer_one_kernel,
        grid=(phases, rows // (INNER * STEP_SUBS * SUB_ROWS)),
        in_specs=[any_spec, w_spec, any_spec, whole, whole],
        out_specs=[out_spec(hid), out_spec(LANES)],
        out_shape=[jax.ShapeDtypeStruct((rows, hid), jnp.bfloat16), jax.ShapeDtypeStruct((rows, LANES), jnp.bfloat16)],
        scratch_shapes=[
            pltpu.VMEM((2 * nodes // phases, LANES), jnp.float32), pltpu.VMEM((rows, hid), jnp.float32),
            *ids, stage, stage, pltpu.VMEM((2, 4096, feat), jnp.bfloat16),
            pltpu.SemaphoreType.DMA((2,)), pltpu.SemaphoreType.DMA((STEP_SUBS // BUF_SUBS,))],
        compiler_params=params(),
        cost_estimate=pl.CostEstimate(flops=2 * 10**11, bytes_accessed=10**8, transcendentals=0),
        name="layer_one")(idx, weights, x_all, w_hidden, w_out_pad)


def layer_two(idx, weights, p_all):
    phases, slots, rows = weights.shape
    any_spec = pl.BlockSpec(memory_space=pl.ANY)
    w_spec, out_spec, ids = forward_specs(weights, phases - 1)
    stage = pltpu.VMEM((slots * SUB_ROWS, LANES), jnp.float32)
    return pl.pallas_call(
        functools.partial(layer_two_kernel, rows),
        grid=(phases, rows // (INNER * STEP_SUBS * SUB_ROWS)),
        in_specs=[any_spec, w_spec, any_spec],
        out_specs=out_spec(LANES),
        out_shape=jax.ShapeDtypeStruct((rows, LANES), jnp.float32),
        scratch_shapes=[
            pltpu.VMEM((2 * rows + 128, LANES), jnp.float32), pltpu.VMEM((rows, LANES), jnp.float32),
            *ids, stage, stage, pltpu.VMEM((2, packed_rows(rows), LANES), jnp.bfloat16),
            pltpu.SemaphoreType.DMA((2,)), pltpu.SemaphoreType.DMA((STEP_SUBS // BUF_SUBS,))],
        compiler_params=params(),
        cost_estimate=pl.CostEstimate(flops=2 * 10**11, bytes_accessed=10**8, transcendentals=0),
        name="layer_two")(idx, weights, p_all)


def segment_product(build, plan, sources, specs, buffers, num_out, width, rows):
    idx, cols, weights, scalars = plan
    phases, edges = cols.shape
    per_step = INNER * STEP_CHUNKS * CHUNK
    steps = edges // per_step
    any_spec = pl.BlockSpec(memory_space=pl.ANY)
    tile_spec = pl.BlockSpec((1, 1, per_step), lambda p, t, *_: (p * steps + t, 0, 0))
    ids = pltpu.SMEM((BUF_CHUNKS * CHUNK,), jnp.int32)
    stage = pltpu.VMEM((width * CHUNK, LANES), jnp.float32)
    grid_spec = pltpu.PrefetchScalarGridSpec(
        num_scalar_prefetch=len(scalars),
        grid=(phases, steps),
        in_specs=[any_spec, tile_spec, tile_spec, *specs],
        out_specs=[any_spec, any_spec],
        scratch_shapes=[
            pltpu.VMEM((width * rows + (128 if width == 1 else 0), LANES), jnp.float32),
            pltpu.VMEM((num_out, width * LANES), jnp.float32),
            pltpu.SMEM((STEP_CHUNKS * CHUNK,), jnp.int32), stage, stage,
            pltpu.SemaphoreType.DMA((STEP_CHUNKS // BUF_CHUNKS,)), pltpu.SemaphoreType.DMA, pltpu.SemaphoreType.DMA((2,)),
            *([ids] * (STEP_CHUNKS // BUF_CHUNKS)), *buffers])
    return pl.pallas_call(
        functools.partial(segment_kernel, width, len(sources), functools.partial(build, rows)),
        grid_spec=grid_spec,
        out_shape=[jax.ShapeDtypeStruct((num_out // 2, width * LANES), jnp.float32)] * 2,
        compiler_params=params(),
        cost_estimate=pl.CostEstimate(flops=2 * 10**11, bytes_accessed=10**8, transcendentals=0))(*scalars, (idx * width).reshape(-1), cols.reshape(phases * steps, 1, per_step),
                   weights.reshape(phases * steps, 1, per_step), *sources)


def edge_lists(cols_blk, mask_blk, vals_blk, col_blocks, blk_nodes, turn):
    slots = cols_blk.shape[0]
    col_nodes = 2 * blk_nodes
    row_ids = lax.broadcasted_iota(jnp.int32, (slots, col_blocks, blk_nodes), 2)
    valid = mask_blk.reshape(slots, col_blocks, blk_nodes) > 0
    turned = jnp.bitwise_xor(cols_blk, turn).reshape(slots, col_blocks, blk_nodes)
    keys = jnp.where(valid, turned, col_nodes) * blk_nodes + row_ids
    weights = jnp.where(valid, vals_blk.reshape(slots, col_blocks, blk_nodes).astype(jnp.float32), 0.0)
    keys = keys.transpose(1, 0, 2).reshape(col_blocks, slots * blk_nodes)
    return keys, weights.transpose(1, 0, 2).reshape(col_blocks, slots * blk_nodes)


def make_plan(keys, weights, blk_nodes):
    col_nodes = 2 * blk_nodes
    cols, rows = keys // blk_nodes, keys % blk_nodes
    chunked = cols.reshape(-1, CHUNK)
    base = jnp.minimum(chunked[:, 0] // 8 * 8, col_nodes - WINDOW)
    last = jnp.max(jnp.where(chunked < col_nodes, chunked, -1), axis=1)
    over = jnp.max((last >= base + WINDOW).astype(jnp.int32).reshape(-1, STEP_CHUNKS), axis=1)
    count = jnp.sum((cols < col_nodes).astype(jnp.int32), axis=1)
    active = jnp.maximum((count + STEP_CHUNKS * CHUNK - 1) // (STEP_CHUNKS * CHUNK), 1)
    return rows, cols, weights, (active, over, base, last)


def all_reduce_kernel(row_size, col_size, x_ref, out_ref, held, send_a, recv_a, send_b, recv_b):
    devices = row_size * col_size
    me = lax.axis_index("row") * col_size + lax.axis_index("col")
    size = x_ref.shape[0] // devices

    def place(index):
        return {"row": index // col_size, "col": index % col_size}

    barrier = pltpu.get_barrier_semaphore()
    for d in range(1, devices):
        pl.semaphore_signal(barrier, inc=1, device_id=place((me + d) % devices), device_id_type=pl.DeviceIdType.MESH)
    pl.semaphore_wait(barrier, devices - 1)
    copies = []
    for d in range(1, devices):
        peer = (me + d) % devices
        copies.append(pltpu.make_async_remote_copy(
            src_ref=x_ref.at[pl.ds(pl.multiple_of(peer * size, size), size), :], dst_ref=held.at[d - 1],
            send_sem=send_a.at[d - 1], recv_sem=recv_a.at[d - 1], device_id=place(peer), device_id_type=pl.DeviceIdType.MESH))
    for copy in copies:
        copy.start()
    for copy in copies:
        copy.wait()
    mine = pl.ds(pl.multiple_of(me * size, size), size)
    total = x_ref[mine, :]
    for d in range(1, devices):
        total = total + held[d - 1]
    out_ref[mine, :] = total
    copies = []
    for d in range(1, devices):
        copies.append(pltpu.make_async_remote_copy(
            src_ref=out_ref.at[mine, :], dst_ref=out_ref.at[mine, :], send_sem=send_b.at[d - 1], recv_sem=recv_b.at[d - 1],
            device_id=place((me + d) % devices), device_id_type=pl.DeviceIdType.MESH))
    for copy in copies:
        copy.start()
    for copy in copies:
        copy.wait()


def all_reduce(x, row_size, col_size):
    devices = row_size * col_size
    whole = pl.BlockSpec(memory_space=pltpu.VMEM)
    sems = pltpu.SemaphoreType.DMA((devices - 1,))
    return pl.pallas_call(
        functools.partial(all_reduce_kernel, row_size, col_size),
        in_specs=[whole],
        out_specs=whole,
        out_shape=jax.ShapeDtypeStruct(x.shape, x.dtype),
        scratch_shapes=[pltpu.VMEM((devices - 1, x.shape[0] // devices, x.shape[1]), x.dtype), sems, sems, sems, sems],
        compiler_params=pltpu.CompilerParams(collective_id=0, has_side_effects=True),
        name="all_reduce")(x)


def solution(mesh):
    row_size = mesh.shape["row"]
    col_size = mesh.shape["col"]
    both_axes = ("row", "col")
    swap = [(0, 1), (1, 0)]

    def device_step(feat_blk, w_hidden, w_output, cols_blk, vals_blk, mask_blk, labels_blk, train_blk):
        row_i, col_j = lax.axis_index("row"), lax.axis_index("col")
        blk_nodes = feat_blk.shape[0]
        col_nodes = blk_nodes * row_size
        packed = packed_rows(blk_nodes)
        slots = cols_blk.shape[0]
        classes = w_output.shape[1]
        any_spec = pl.BlockSpec(memory_space=pl.ANY)
        whole = pl.BlockSpec(memory_space=pltpu.VMEM)
        w_out_pad = jnp.pad(w_output, ((0, 0), (0, LANES - classes)))

        x_all = lax.all_gather(feat_blk, both_axes, axis=0, tiled=True)
        masked = vals_blk * mask_blk.astype(jnp.bfloat16)
        own_cols = lax.all_to_all(cols_blk, "col", split_axis=1, concat_axis=0, tiled=True)
        own_w = lax.all_to_all(masked, "col", split_axis=1, concat_axis=0, tiled=True)
        own_w = own_w.astype(jnp.float32).reshape(col_size, slots, blk_nodes)
        own_cols = own_cols.reshape(col_size, slots, -1, STEP_SUBS, SUB_ROWS).transpose(0, 2, 3, 1, 4).reshape(-1)

        keys, edge_w = edge_lists(cols_blk, mask_blk, vals_blk, col_size, blk_nodes, (1 - row_i) * blk_nodes)
        edges = lax.sort((keys, edge_w), dimension=1, num_keys=1, is_stable=False)
        x_all, edges = lax.optimization_barrier((x_all, edges))
        plan = make_plan(*edges, blk_nodes)

        z_one, proj_two = layer_one(own_cols * 2, own_w, x_all, w_hidden, w_out_pad)
        count = jnp.sum(train_blk)
        spare = PACK * pack_lanes()
        lane_ids = lax.broadcasted_iota(jnp.int32, (packed, LANES), 1)
        counts = jnp.where(lane_ids == spare, count // 128, jnp.where(lane_ids == spare + 1, count % 128, 0))
        p_all = lax.all_gather(pack_nodes(proj_two[:, :classes]) + counts.astype(jnp.bfloat16), both_axes, axis=0, tiled=True)
        z_one, p_all = lax.optimization_barrier((z_one, p_all))
        z_first = lax.all_gather(z_one[:blk_nodes // 2], "col", axis=0, tiled=True)
        counts = p_all.reshape(row_size * col_size, packed, LANES)[:, 0, spare:spare + 2].astype(jnp.float32)
        train_count = jnp.maximum(jnp.sum(counts[:, 0] * 128.0 + counts[:, 1]), 1.0)
        z_two = layer_two(own_cols, own_w, p_all)[:, :classes]

        mask_f = train_blk.astype(jnp.float32)
        log_norm = jax.nn.logsumexp(z_two, axis=1)
        onehot = (labels_blk[:, None] == jnp.arange(classes, dtype=jnp.int32)[None, :]).astype(jnp.float32)
        picked = jnp.sum(z_two * onehot, axis=1)
        loss_mean = jnp.sum(mask_f * (log_norm - picked)) / train_count
        softmax_z = jnp.exp(z_two - log_norm[:, None])
        grad_two = ((mask_f / train_count)[:, None] * (softmax_z - onehot)).astype(jnp.bfloat16)
        z_first, grad_two = lax.optimization_barrier((z_first, grad_two))
        grad_rows = lax.all_gather(pack_nodes(grad_two), "col", axis=0, tiled=True)
        z_later, grad_rows = lax.optimization_barrier((z_one[blk_nodes // 2:], grad_rows))
        z_second = lax.all_gather(z_later, "col", axis=0, tiled=True)

        row_bufs = [pltpu.VMEM((1, packed, LANES), jnp.bfloat16), pltpu.SemaphoreType.DMA((1,))]
        send_two, keep_two = segment_product(
            build_packed, plan, [grad_rows], [any_spec], row_bufs, col_nodes, 1, blk_nodes)
        back_two = (keep_two + lax.ppermute(send_two, "row", swap)).astype(jnp.bfloat16)
        z_second, back_two = lax.optimization_barrier((z_second, back_two))
        back_all = lax.all_gather(pack_nodes(back_two[:, :classes]), ("col", "row"), axis=0, tiled=True)
        back_rows = lax.dynamic_slice_in_dim(back_all, row_i * col_size * packed, col_size * packed, 0)
        back_own = lax.dynamic_slice_in_dim(back_rows, col_j * packed, packed, 0)
        back_own = jnp.concatenate([back_own[:, q * pack_lanes():q * pack_lanes() + classes] for q in range(PACK)], axis=0)[:blk_nodes]
        h_one = jnp.maximum(z_one, 0)
        grad_w_output = lax.dot_general(h_one, back_own, CONTRACT_ROWS, preferred_element_type=jnp.float32)

        send_one, keep_one = segment_product(
            build_dz, plan, [z_first, z_second, back_rows, w_out_pad], [any_spec, any_spec, any_spec, whole],
            [pltpu.VMEM((2, 4, 1024, 2 * LANES), jnp.bfloat16), pltpu.SemaphoreType.DMA((2, 4)), *row_bufs,
             pltpu.VMEM((blk_nodes + 128, LANES), jnp.bfloat16)],
            col_nodes, 2, blk_nodes)
        back_one = (keep_one + lax.ppermute(send_one, "row", swap)).astype(jnp.bfloat16)
        feat_src = lax.dynamic_slice_in_dim(x_all, (col_j * row_size + row_i) * blk_nodes, blk_nodes, 0)
        grad_w_hidden = lax.dot_general(feat_src, back_one, CONTRACT_ROWS, preferred_element_type=jnp.float32)
        feat, hid = w_hidden.shape
        out_pad = jnp.pad(grad_w_output, ((0, 0), (0, LANES - classes)))
        rows = feat * hid // LANES + hid
        packed_out = jnp.concatenate([grad_w_hidden.reshape(-1, LANES), out_pad, jnp.full((1, LANES), loss_mean)], axis=0)
        unit = 8 * row_size * col_size
        packed_out = jnp.pad(packed_out, ((0, -(rows + 1) % unit), (0, 0)))
        total = all_reduce(packed_out, row_size, col_size)
        grad_w_hidden = total[:feat * hid // LANES].reshape(feat, hid)
        return total[rows, 0], grad_w_hidden, total[feat * hid // LANES:rows, :classes]

    node_spec = P(("row", "col"), None)
    label_spec = P(("row", "col"))
    adj_spec = P("col", "row")
    return jax.shard_map(device_step, mesh=mesh, in_specs=(node_spec, P(), P(), adj_spec, adj_spec, adj_spec, label_spec, label_spec), out_specs=(P(), P(), P()), check_vma=False)
```

time: 1750 us -> 1580 us (0.903)
  Pallas kernels: 1080 us -> 1010 us
  blocking collectives: 51 us -> 0 us
  waiting for transfers between devices: 260 us -> 209 us
    pallas_call x2, Pallas kernels: 562 us -> 490 us  [segment_product(): pl.pallas_call(functools.partial(segment_kernel, width, len(sources), fun...]
    psum x2 -> x0, blocking collectives: 51 us -> none  [the longest x1 26.7 us: device_step(): lax.psum(jnp.sum(train_blk), both_axes)]
    all_gather x2 -> x3, waiting for transfers between devices: 95.8 us -> 60.8 us  [the longest x1 60.8 us: device_step(): lax.all_gather(pack_nodes(proj_two[:, :classes]) + counts.astype(jnp.bflo...]
    pallas_call x1 -> x2, Pallas kernels: 284 us -> 302 us  [the longest x1 277 us: layer_one(): pl.pallas_call(layer_one_kernel, grid=(phases, rows // (INNER * STEP_SUBS...]
  transfers between devices with their start and end apart: 10 -> 10, of which waited for: 8 -> 6; matrix products, arithmetic and copies ran while one was open for 15% -> 17% of each run, Pallas kernels for 13% -> 28%
where the time goes in v3:
time: 1580 us; the launch traced here: 1570 us
  Pallas kernels  1010 us (64%)
  other arithmetic  246 us (16%)
  waiting for transfers between devices  209 us (13%)
  local copies, waits for them, and re-layouts  54.1 us (3%)
  matrix products  19.4 us (1%)
  between operations  18.9 us (1%)
    pallas_call x2, Pallas kernels, segment_product(): pl.pallas_call(functools.partial(segment_kernel, width, len(sources), fun...  490 us
    pallas_call x1, Pallas kernels, layer_one(): pl.pallas_call(layer_one_kernel, grid=(phases, rows // (INNER * STEP_SUBS...  277 us
    pallas_call x1, Pallas kernels, layer_two(): pl.pallas_call(functools.partial(layer_two_kernel, rows), grid=(phases, r...  218 us
    sort x1, other arithmetic, device_step(): edges = lax.sort((keys, edge_w), dimension=1, num_keys=1, is_stable=False)  192 us
    all_gather x1, waiting for transfers between devices, device_step(): lax.all_gather(pack_nodes(back_two[:, :classes]), ('col', 'row'), axis=0,...  70.6 us
    all_gather x1, waiting for transfers between devices, device_step(): lax.all_gather(pack_nodes(proj_two[:, :classes]) + counts.astype(jnp.bflo...  60.8 us
    all_gather x1, waiting for transfers between devices, device_step(): grad_rows = lax.all_gather(pack_nodes(grad_two), 'col', axis=0, tiled=True)  46.2 us
  transfers between devices with their start and end apart: 10, of which 6 were waited for; matrix products, arithmetic and copies ran while one was open for 17% of the time, Pallas kernels for 28%

profile of v3, /device:TPU:0, one launch (start us, length us, event | category | flops | bytes accessed | tf_op | source)
XLA Modules:
  0.0 1568.1 jit_solution(15310144674233811935)
XLA Ops:
  7.2 0.7 all-gather.7.cloned.1.call-update
  8.6 1.1 convert_multiply_fusion
  9.7 5.5 all-to-all-start.1
  15.7 2.0 select_multiply_fusion
  17.7 0.9 mul.68
  18.8 0.6 reduce_sum.55
  22.1 0.9 select_n.85
  23.2 192.5 %sort.15 = (s32[4,65536]{1,0:T(4,128)}, f32[4,65536]{1,0:T(4,128)}) sort(s32[4,65536]{1,0:T(4,128)S(1)} %bitcast.33, f32[4,65536]{1,0:T(4,128)S(1)} %bitcast.34), dimensions={1}, to_apply=%region_0.1 | sort | flops 4718592 | bytes 4194304 | tf_op jit(solution)/shard_map/sort | solution.py:584
  215.6 0.6 pad.32.w_output.refs_3_
  217.3 4.2 all-to-all-start
  221.5 2.1 convert_bitcast_fusion.w_ref
  223.6 11.5 all-to-all-done
  235.2 0.9 reshape.91
  236.1 0.7 copy.29
  236.8 0.5 copy.41
  237.3 1.0 copy-done.3
  238.3 1.1 broadcast_multiply_fusion.idx_hbm
  239.4 277.2 %layer_one.1 = (bf16[16384,256]{1,0:T(8,128)(2,1)}, bf16[16384,128]{1,0:T(8,128)(2,1)}) custom-call(s32[262144]{0:T(1024)} %broadcast_multiply_fusion.idx_hbm, f32[4,4,16384]{2,1,0:T(4,128)} %convert_bitcast_fusion.w_ref, bf16[131072,128]{1,0:T(8,128)(2,1)} %all-gather.7.cloned.1.call-done.x_hbm, bf16[128,256]{1,0:T(8,128)(2,1)} %w_hidden.1, ...), custom_call_target="tpu_custom_call" | custom-call | flops 199999995904 | bytes 100000000 | tf_op jit(solution)/shard_map/layer_one/pallas_call | solution.py:419
  516.6 2.6 fusion.44
  519.2 2.7 fusion.14
  522.0 60.8 %all-gather.9.cloned.1.call-done.p_hbm = bf16[43776,128]{1,0:T(8,128)(2,1)} async-done(((bf16[5472,128]{1,0:T(8,128)(2,1)}), bf16[43776,128]{1,0:T(8,128)(2,1)}) %all-gather.9.cloned.1.call-update) | async-done | bytes 11206672 | tf_op jit(solution)/shard_map/all_gather | solution.py:593
  582.8 5.7 fusion.41
  588.6 0.8 slice.111
  589.5 0.6 add_reduce_fusion
  590.7 217.9 %layer_two.1 = f32[16384,128]{1,0:T(8,128)} custom-call(s32[262144]{0:T(1024)} %bitcast.32, f32[4,4,16384]{2,1,0:T(4,128)} %convert_bitcast_fusion.w_ref, bf16[43776,128]{1,0:T(8,128)(2,1)} %all-gather.9.cloned.1.call-done.p_hbm), custom_call_target="tpu_custom_call" | custom-call | flops 199999995904 | bytes 100000000 | tf_op jit(solution)/shard_map/layer_two/pallas_call | solution.py:439
  808.7 5.6 slice_reduce_fusion
  814.5 10.2 select_reduce_fusion
  824.8 0.6 multiply_reduce_fusion
  825.4 8.5 multiply_convert_fusion
  834.0 2.6 fusion.43
  836.5 2.6 fusion.20
  839.4 3.3 multiply_bitcast_fusion
  842.7 0.7 reshape.87
  843.4 2.4 reshape.89.col_ref
  846.6 1.1 copy.42
  847.7 2.4 reshape.90.w_ref
  850.1 0.7 convert_reduce_fusion.1.over_ref
  851.3 0.6 fusion.35.base_ref
  851.9 46.2 %all-gather.13.cloned.1.call-done.refs_0_ = bf16[21888,128]{1,0:T(8,128)(2,1)} async-done(((bf16[5472,128]{1,0:T(8,128)(2,1)}), bf16[21888,128]{1,0:T(8,128)(2,1)}) %all-gather.13.cloned.1.call-update) | async-done | bytes 5603344 | tf_op jit(solution)/shard_map/all_gather | solution.py:608
  898.3 225.1 %shard_map.103 = (f32[16384,128]{1,0:T(8,128)}, f32[16384,128]{1,0:T(8,128)}) custom-call(s32[4]{0:T(128)} %fusion.38.active_ref, s32[64]{0:T(128)} %convert_reduce_fusion.1.over_ref, s32[1024]{0:T(1024)} %fusion.35.base_ref, s32[1024]{0:T(1024)} %copy-done.12, s32[262144]{0:T(1024)} %bitcast.38, s32[16,1,16384]{2,1,0:T(1,128)} %reshape.89.col_ref, ...), custom_call_target="tpu_custom_call" | custom-call | flops 199999995904 | bytes 100000000 | tf_op jit(solution)/shard_map/pallas_call | solution.py:474
  1123.5 13.4 collective-permute-done
  1136.9 5.4 add_convert_fusion.2
  1142.3 2.1 fusion.42
  1144.4 0.9 copy-done.1
  1145.6 2.7 fusion.18
  1148.3 1.0 copy.43
  1149.4 70.6 %all-gather.17.cloned.1.call-done = bf16[43776,128]{1,0:T(8,128)(2,1)} async-done(((bf16[5472,128]{1,0:T(8,128)(2,1)}), bf16[43776,128]{1,0:T(8,128)(2,1)}) %all-gather.17.cloned.1.call-update) | async-done | bytes 11206672 | tf_op jit(solution)/shard_map/all_gather | solution.py:617
  1219.9 6.0 constant_dynamic-slice_fusion.1.refs_2_
  1226.0 265.1 %shard_map.104 = (f32[16384,256]{1,0:T(8,128)}, f32[16384,256]{1,0:T(8,128)}) custom-call(s32[4]{0:T(128)} %fusion.38.active_ref, s32[64]{0:T(128)} %convert_reduce_fusion.1.over_ref, s32[1024]{0:T(1024)} %fusion.35.base_ref, s32[1024]{0:T(1024)} %copy-done.12, s32[262144]{0:T(1024)} %bitcast.39, s32[16,1,16384]{2,1,0:T(1,128)} %reshape.89.col_ref, ...), custom_call_target="tpu_custom_call" | custom-call | flops 199999995904 | bytes 100000000 | tf_op jit(solution)/shard_map/pallas_call | solution.py:474
  1492.0 4.9 fusion.40
  1496.9 1.8 copy.32
  1498.7 1.8 copy.33
  1500.4 1.2 copy.34
  1501.6 3.5 concatenate.18
  1505.1 5.7 fusion.1
  1510.9 5.7 collective-permute-done.1
  1516.6 13.6 fusion
  1530.4 0.7 pad.40.x_ref
  1531.1 25.2 %all_reduce.1 = f32[576,128]{1,0:T(8,128)} custom-call(f32[576,128]{1,0:T(8,128)} %pad.40.x_ref), custom_call_target="tpu_custom_call" | custom-call | tf_op jit(solution)/shard_map/all_reduce/pallas_call | solution.py:549
  1556.3 1.2 slice.107
  1557.5 0.9 slice.108
  1558.4 0.9 slice.109
  1559.3 0.7 reshape.96
  1560.0 0.7 copy.36
  (63 shorter events, 5.6 us)
Async XLA Ops:
  7.2 1.0 copy-start.5
  7.2 1.4 copy-start.4
  7.2 232.2 %all-gather.7.cloned.1.call-start = ((), (), s32[]{:S(2)}) async-start(), calls=%async_computation.2 | async-start | bytes 37748736 | tf_op jit(solution)/shard_map/all_gather | solution.py:576
  9.7 207.7 %all-to-all-start.1 = ((bf16[4,4,16384]{2,0,1:T(4,128)(2,1)}), bf16[4,4,16384]{2,0,1:T(4,128)(2,1)}, u32[]{:S(2)}, u32[]{:S(2)}) async-start(bf16[4,4,16384]{2,0,1:T(4,128)(2,1)} %bitcast.8), calls=%async_computation.1 | async-start | bytes 1048576 | tf_op jit(solution)/shard_map/all_to_all | solution.py:579
  15.7 3.1 copy-start.9
  17.7 5.3 copy-start.11
  217.3 17.9 %all-to-all-start = ((s32[4,4,16384]{2,0,1:T(4,128)}), s32[4,4,16384]{2,0,1:T(4,128)S(1)}, u32[]{:S(2)}, u32[]{:S(2)}) async-start(s32[4,4,16384]{2,0,1:T(4,128)} %bitcast.5), calls=%async_computation | async-start | bytes 2097152 | tf_op jit(solution)/shard_map/all_to_all | solution.py:578
  221.5 361.2 %all-gather.9.cloned.1.call-start = ((), (), s32[]{:S(2)}) async-start(), calls=%async_computation.3 | async-start | bytes 12607488 | tf_op jit(solution)/shard_map/all_gather | solution.py:593
  237.3 1.0 copy-start.3
  516.6 2.6 copy-start.13
  516.6 2.6 copy-start.14
  522.0 312.0 %all-gather.11.cloned.1.call-start = ((), (), s32[]{:S(2)}) async-start(), calls=%async_computation.4 | async-start | bytes 20971520 | tf_op jit(solution)/shard_map/all_gather | solution.py:595
  588.5 309.5 %all-gather.13.cloned.1.call-start = ((), (), s32[]{:S(2)}) async-start(), calls=%async_computation.5 | async-start | bytes 7004160 | tf_op jit(solution)/shard_map/all_gather | solution.py:608
  808.7 5.8 copy-start
  808.7 5.8 copy-start.8
  814.5 10.2 copy-start.10
  836.5 2.9 copy-start.6
  839.2 303.1 %all-gather.15.cloned.1.call-start = ((), (), s32[]{:S(2)}) async-start(), calls=%async_computation.6 | async-start | bytes 20971520 | tf_op jit(solution)/shard_map/all_gather | solution.py:610
  846.0 4.0 copy-start.12
  846.3 1.3 copy-start.7
  898.1 321.9 %all-gather.17.cloned.1.call-start = ((), (), s32[]{:S(2)}) async-start(), calls=%async_computation.7 | async-start | bytes 12607488 | tf_op jit(solution)/shard_map/all_gather | solution.py:617
  1123.5 13.4 collective-permute-start
  1142.3 3.0 copy-start.1
  1145.6 2.7 copy-start.2
  1491.1 25.5 %collective-permute-start.1 = (f32[16384,256]{1,0:T(8,128)}, f32[16384,256]{1,0:T(8,128)}, u32[]{:S(2)}, u32[]{:S(2)}) collective-permute-start(f32[16384,256]{1,0:T(8,128)} %get-tuple-element.40), channel_id=1, source_target_pairs={{0,1},{1,0},{2,3},{3,2},{4,5},{5,4},{6,7},{7,6}} | collective-permute-start | bytes 50331656 | tf_op jit(solution)/shard_map/ppermute | solution.py:629
Sparse Core Ops, SparseCore 0:
  9.8 157.9 all-gather.6
  522.1 60.6 all-gather.8
  588.7 151.7 all-gather.10
  839.3 58.7 all-gather.12
  899.7 151.7 all-gather.14
  1148.4 71.4 all-gather.16

commit v4 on v3

--- a/solution.py
+++ b/solution.py
@@ -227,8 +227,26 @@
     return jnp.pad(jnp.concatenate(parts, axis=1), ((0, 0), (0, LANES - PACK * pack_lanes())))
 
 
-def layer_two_kernel(nodes, idx_hbm, w_ref, p_hbm, z_ref, table, acc, ids_a, ids_b, ids_c, ids_d, stage_a, stage_b, p_buf, sems, idx_sems):
+def pack_rows(acc, first, piece, packed, n):
+    lane = lax.broadcasted_iota(jnp.int32, (piece, LANES), 1)
+    total = None
+    for q in range(PACK):
+        rows = acc[pl.ds(pl.multiple_of(first + q * packed + n * piece, 8), piece), :]
+        rows = jnp.where(lane < pack_lanes(), rows, 0.0)
+        rows = rows if q == 0 else pltpu.roll(rows, q * pack_lanes(), 1)
+        total = rows if q == 0 else total + rows
+    return total
+
+
+def layer_two_kernel(nodes, classes, idx_hbm, w_ref, p_hbm, node_ref, count_ref, grad_ref, loss_ref, table, acc, ids_a, ids_b,
+                     ids_c, ids_d, stage_a, stage_b, p_buf, sems, idx_sems):
     phase, tile = pl.program_id(0), pl.program_id(1)
+    packed = packed_rows(nodes)
+
+    @pl.when((phase == 0) & (tile == 0))
+    def _():
+        acc[nodes:, :] = jnp.zeros((acc.shape[0] - nodes, LANES), jnp.float32)
+        loss_ref[...] = jnp.zeros_like(loss_ref)
 
     @pl.when(tile == 0)
     def _():
@@ -238,17 +256,46 @@
 
     @pl.when(phase == pl.num_programs(0) - 1)
     def _():
-        def use(at, sums):
-            z_ref[at, :] = sums
-
-        finish_rows(acc, use)
-
-
-def segment_kernel(width, n_src, build, active_ref, over_ref, base_ref, last_ref, idx_hbm, col_ref, w_ref, *refs):
+        size = INNER * STEP_SUBS * SUB_ROWS
+        group = 512
+        lane = lax.broadcasted_iota(jnp.int32, (group, LANES), 1)
+        lane_f = lane.astype(jnp.float32)
+        count = count_ref[0]
+
+        def body(n, carry):
+            rows = pl.ds(pl.multiple_of(tile * size + n * group, group), group)
+            columns = node_ref[:, rows].T
+            label = jnp.broadcast_to(columns[:, 0:1], (group, LANES))
+            mask = jnp.broadcast_to(columns[:, 1:2], (group, LANES))
+            z_two = jnp.where(lane < classes, acc[rows, :], -jnp.inf)
+            top = jnp.max(z_two, axis=1, keepdims=True)
+            log_norm = jnp.log(jnp.sum(jnp.exp(z_two - top), axis=1, keepdims=True)) + top
+            hit = lane_f == label
+            terms = mask * (jnp.where(lane == 0, log_norm, 0.0) - jnp.where(hit, z_two, 0.0))
+            loss_ref[...] += jnp.sum(terms.reshape(group // 8, 8, LANES), axis=0)
+            acc[rows, :] = (mask / count) * (jnp.exp(z_two - log_norm) - jnp.where(hit, 1.0, 0.0))
+            return carry
+
+        lax.fori_loop(0, size // group, body, 0)
+
+    @pl.when((phase == pl.num_programs(0) - 1) & (tile == pl.num_programs(1) - 1))
+    def _():
+        piece = packed // 18
+
+        def body(n, carry):
+            grad_ref[pl.ds(pl.multiple_of(n * piece, 16), piece), :] = pack_rows(acc, 0, piece, packed, n).astype(jnp.bfloat16)
+            return carry
+
+        lax.fori_loop(0, 18, body, 0)
+
+
+def segment_kernel(width, nodes, n_src, build, active_ref, over_ref, base_ref, last_ref, idx_hbm, col_ref, w_ref, *refs):
     bufs = STEP_CHUNKS // BUF_CHUNKS
     sources, refs = refs[:n_src], refs[n_src:]
     (out_first, out_second, table, acc, spare_ids, stage_a, stage_b, idx_sems, spare_sem, out_sems), refs = refs[:10], refs[10:]
     ids, refs = refs[:bufs], refs[bufs:]
+    if width == 1:
+        packed_sums, refs = refs[0], refs[1:]
     buffers, sems = refs[0::2], refs[1::2]
     stages = [stage_a, stage_b]
     phase, tile = pl.program_id(0), pl.program_id(1)
@@ -361,9 +408,22 @@
 
     @pl.when((phase == pl.num_programs(0) - 1) & (tile == pl.num_programs(1) - 1))
     def _():
-        half = acc.shape[0] // 2
-        copies = [pltpu.make_async_copy(acc.at[pl.ds(n * half, half), :], out, out_sems.at[n])
-                  for n, out in enumerate([out_first, out_second])]
+        half = nodes
+        if width == 1:
+            packed = packed_rows(nodes)
+            piece = packed // 18
+            for part in range(2):
+                def body(n, carry):
+                    at = pl.ds(pl.multiple_of(n * piece, 8), piece)
+                    packed_sums[part, at, :] = pack_rows(acc, part * half, piece, packed, n)
+                    return carry
+
+                lax.fori_loop(0, 18, body, 0)
+            results = [packed_sums.at[0], packed_sums.at[1]]
+        else:
+            results = [acc.at[pl.ds(part * half, half), :] for part in range(2)]
+        copies = [pltpu.make_async_copy(result, out, out_sems.at[n])
+                  for n, (result, out) in enumerate(zip(results, [out_first, out_second]))]
         for copy in copies:
             copy.start()
         for copy in copies:
@@ -431,35 +491,37 @@
         name="layer_one")(idx, weights, x_all, w_hidden, w_out_pad)
 
 
-def layer_two(idx, weights, p_all):
+def layer_two(idx, weights, p_all, node_rows, count, classes):
     phases, slots, rows = weights.shape
     any_spec = pl.BlockSpec(memory_space=pl.ANY)
-    w_spec, out_spec, ids = forward_specs(weights, phases - 1)
+    whole = pl.BlockSpec(memory_space=pltpu.VMEM)
+    w_spec, _, ids = forward_specs(weights, phases - 1)
     stage = pltpu.VMEM((slots * SUB_ROWS, LANES), jnp.float32)
     return pl.pallas_call(
-        functools.partial(layer_two_kernel, rows),
+        functools.partial(layer_two_kernel, rows, classes),
         grid=(phases, rows // (INNER * STEP_SUBS * SUB_ROWS)),
-        in_specs=[any_spec, w_spec, any_spec],
-        out_specs=out_spec(LANES),
-        out_shape=jax.ShapeDtypeStruct((rows, LANES), jnp.float32),
+        in_specs=[any_spec, w_spec, any_spec, whole, pl.BlockSpec(memory_space=pltpu.SMEM)],
+        out_specs=[whole, whole],
+        out_shape=[jax.ShapeDtypeStruct((packed_rows(rows), LANES), jnp.bfloat16), jax.ShapeDtypeStruct((8, LANES), jnp.float32)],
         scratch_shapes=[
-            pltpu.VMEM((2 * rows + 128, LANES), jnp.float32), pltpu.VMEM((rows, LANES), jnp.float32),
+            pltpu.VMEM((2 * rows + 128, LANES), jnp.float32), pltpu.VMEM((rows + 128, LANES), jnp.float32),
             *ids, stage, stage, pltpu.VMEM((2, packed_rows(rows), LANES), jnp.bfloat16),
             pltpu.SemaphoreType.DMA((2,)), pltpu.SemaphoreType.DMA((STEP_SUBS // BUF_SUBS,))],
         compiler_params=params(),
         cost_estimate=pl.CostEstimate(flops=2 * 10**11, bytes_accessed=10**8, transcendentals=0),
-        name="layer_two")(idx, weights, p_all)
+        name="layer_two")(idx, weights, p_all, node_rows, count)
 
 
 def segment_product(build, plan, sources, specs, buffers, num_out, width, rows):
-    idx, cols, weights, scalars = plan
-    phases, edges = cols.shape
-    per_step = INNER * STEP_CHUNKS * CHUNK
-    steps = edges // per_step
+    ids_by_width, cols, weights, scalars = plan
+    phases = scalars[0].shape[0]
+    steps, per_step = cols.shape[0] // phases, cols.shape[2]
     any_spec = pl.BlockSpec(memory_space=pl.ANY)
     tile_spec = pl.BlockSpec((1, 1, per_step), lambda p, t, *_: (p * steps + t, 0, 0))
     ids = pltpu.SMEM((BUF_CHUNKS * CHUNK,), jnp.int32)
     stage = pltpu.VMEM((width * CHUNK, LANES), jnp.float32)
+    out_rows = packed_rows(rows) if width == 1 else num_out // 2
+    sums = [pltpu.VMEM((2, out_rows, LANES), jnp.float32)] if width == 1 else []
     grid_spec = pltpu.PrefetchScalarGridSpec(
         num_scalar_prefetch=len(scalars),
         grid=(phases, steps),
@@ -467,17 +529,16 @@
         out_specs=[any_spec, any_spec],
         scratch_shapes=[
             pltpu.VMEM((width * rows + (128 if width == 1 else 0), LANES), jnp.float32),
-            pltpu.VMEM((num_out, width * LANES), jnp.float32),
+            pltpu.VMEM((num_out + (256 if width == 1 else 0), width * LANES), jnp.float32),
             pltpu.SMEM((STEP_CHUNKS * CHUNK,), jnp.int32), stage, stage,
             pltpu.SemaphoreType.DMA((STEP_CHUNKS // BUF_CHUNKS,)), pltpu.SemaphoreType.DMA, pltpu.SemaphoreType.DMA((2,)),
-            *([ids] * (STEP_CHUNKS // BUF_CHUNKS)), *buffers])
+            *([ids] * (STEP_CHUNKS // BUF_CHUNKS)), *sums, *buffers])
     return pl.pallas_call(
-        functools.partial(segment_kernel, width, len(sources), functools.partial(build, rows)),
+        functools.partial(segment_kernel, width, rows, len(sources), functools.partial(build, rows)),
         grid_spec=grid_spec,
-        out_shape=[jax.ShapeDtypeStruct((num_out // 2, width * LANES), jnp.float32)] * 2,
+        out_shape=[jax.ShapeDtypeStruct((out_rows, width * LANES), jnp.float32)] * 2,
         compiler_params=params(),
-        cost_estimate=pl.CostEstimate(flops=2 * 10**11, bytes_accessed=10**8, transcendentals=0))(*scalars, (idx * width).reshape(-1), cols.reshape(phases * steps, 1, per_step),
-                   weights.reshape(phases * steps, 1, per_step), *sources)
+        cost_estimate=pl.CostEstimate(flops=2 * 10**11, bytes_accessed=10**8, transcendentals=0))(*scalars, ids_by_width[width - 1], cols, weights, *sources)
 
 
 def edge_lists(cols_blk, mask_blk, vals_blk, col_blocks, blk_nodes, turn):
@@ -501,7 +562,9 @@
     over = jnp.max((last >= base + WINDOW).astype(jnp.int32).reshape(-1, STEP_CHUNKS), axis=1)
     count = jnp.sum((cols < col_nodes).astype(jnp.int32), axis=1)
     active = jnp.maximum((count + STEP_CHUNKS * CHUNK - 1) // (STEP_CHUNKS * CHUNK), 1)
-    return rows, cols, weights, (active, over, base, last)
+    tiles = (-1, 1, INNER * STEP_CHUNKS * CHUNK)
+    ids_by_width = (rows.reshape(-1), 2 * rows.reshape(-1))
+    return ids_by_width, cols.reshape(tiles), weights.reshape(tiles), (active, over, base, last)
 
 
 def all_reduce_kernel(row_size, col_size, x_ref, out_ref, held, send_a, recv_a, send_b, recv_b):
@@ -591,21 +654,16 @@
         lane_ids = lax.broadcasted_iota(jnp.int32, (packed, LANES), 1)
         counts = jnp.where(lane_ids == spare, count // 128, jnp.where(lane_ids == spare + 1, count % 128, 0))
         p_all = lax.all_gather(pack_nodes(proj_two[:, :classes]) + counts.astype(jnp.bfloat16), both_axes, axis=0, tiled=True)
-        z_one, p_all = lax.optimization_barrier((z_one, p_all))
+        z_one, p_all, plan = lax.optimization_barrier((z_one, p_all, plan))
         z_first = lax.all_gather(z_one[:blk_nodes // 2], "col", axis=0, tiled=True)
         counts = p_all.reshape(row_size * col_size, packed, LANES)[:, 0, spare:spare + 2].astype(jnp.float32)
         train_count = jnp.maximum(jnp.sum(counts[:, 0] * 128.0 + counts[:, 1]), 1.0)
-        z_two = layer_two(own_cols, own_w, p_all)[:, :classes]
-
-        mask_f = train_blk.astype(jnp.float32)
-        log_norm = jax.nn.logsumexp(z_two, axis=1)
-        onehot = (labels_blk[:, None] == jnp.arange(classes, dtype=jnp.int32)[None, :]).astype(jnp.float32)
-        picked = jnp.sum(z_two * onehot, axis=1)
-        loss_mean = jnp.sum(mask_f * (log_norm - picked)) / train_count
-        softmax_z = jnp.exp(z_two - log_norm[:, None])
-        grad_two = ((mask_f / train_count)[:, None] * (softmax_z - onehot)).astype(jnp.bfloat16)
+        node_rows = jnp.zeros((8, blk_nodes), jnp.float32)
+        node_rows = node_rows.at[0].set(labels_blk.astype(jnp.float32)).at[1].set(train_blk.astype(jnp.float32))
+        grad_two, loss = layer_two(own_cols, own_w, p_all, node_rows, train_count.reshape(1), classes)
+        loss_mean = jnp.sum(loss) / train_count
         z_first, grad_two = lax.optimization_barrier((z_first, grad_two))
-        grad_rows = lax.all_gather(pack_nodes(grad_two), "col", axis=0, tiled=True)
+        grad_rows = lax.all_gather(grad_two, "col", axis=0, tiled=True)
         z_later, grad_rows = lax.optimization_barrier((z_one[blk_nodes // 2:], grad_rows))
         z_second = lax.all_gather(z_later, "col", axis=0, tiled=True)
 
@@ -614,7 +672,7 @@
             build_packed, plan, [grad_rows], [any_spec], row_bufs, col_nodes, 1, blk_nodes)
         back_two = (keep_two + lax.ppermute(send_two, "row", swap)).astype(jnp.bfloat16)
         z_second, back_two = lax.optimization_barrier((z_second, back_two))
-        back_all = lax.all_gather(pack_nodes(back_two[:, :classes]), ("col", "row"), axis=0, tiled=True)
+        back_all = lax.all_gather(back_two, ("col", "row"), axis=0, tiled=True)
         back_rows = lax.dynamic_slice_in_dim(back_all, row_i * col_size * packed, col_size * packed, 0)
         back_own = lax.dynamic_slice_in_dim(back_rows, col_j * packed, packed, 0)
         back_own = jnp.concatenate([back_own[:, q * pack_lanes():q * pack_lanes() + classes] for q in range(PACK)], axis=0)[:blk_nodes]

time: 1580 us -> 1560 us (0.987)
  other arithmetic: 246 us -> 214 us
  Pallas kernels: 1010 us -> 1030 us
    pallas_call x3, Pallas kernels: 708 us -> 731 us  [the longest x2 492 us: segment_product(): pl.pallas_call(functools.partial(segment_kernel, width, rows, len(sources...]
  transfers between devices with their start and end apart: 10 -> 10, of which waited for: 6 -> 6; matrix products, arithmetic and copies ran while one was open for 17% -> 16% of each run, Pallas kernels for 28% -> 30%
where the time goes in v4:
time: 1560 us; the launch traced here: 1550 us
  Pallas kernels  1030 us (66%)
  other arithmetic  214 us (14%)
  waiting for transfers between devices  200 us (13%)
  local copies, waits for them, and re-layouts  49.5 us (3%)
  matrix products  19.4 us (1%)
  between operations  18.9 us (1%)
    pallas_call x2, Pallas kernels, segment_product(): pl.pallas_call(functools.partial(segment_kernel, width, rows, len(sources...  492 us
    pallas_call x1, Pallas kernels, layer_one(): pl.pallas_call(layer_one_kernel, grid=(phases, rows // (INNER * STEP_SUBS...  277 us
    pallas_call x1, Pallas kernels, layer_two(): pl.pallas_call(functools.partial(layer_two_kernel, rows, classes), grid=(...  239 us
    sort x1, other arithmetic, device_step(): edges = lax.sort((keys, edge_w), dimension=1, num_keys=1, is_stable=False)  193 us
    all_gather x1, waiting for transfers between devices, device_step(): back_all = lax.all_gather(back_two, ('col', 'row'), axis=0, tiled=True)  71.6 us
    all_gather x1, waiting for transfers between devices, device_step(): grad_rows = lax.all_gather(grad_two, 'col', axis=0, tiled=True)  58.8 us
    all_gather x1, waiting for transfers between devices, device_step(): lax.all_gather(pack_nodes(proj_two[:, :classes]) + counts.astype(jnp.bflo...  47 us
  transfers between devices with their start and end apart: 10, of which 6 were waited for; matrix products, arithmetic and copies ran while one was open for 16% of the time, Pallas kernels for 30%

profile of v4, /device:TPU:0, one launch (start us, length us, event | category | flops | bytes accessed | tf_op | source)
XLA Modules:
  0.0 1546.0 jit_solution(16741864695748423902)
XLA Ops:
  7.2 0.7 all-gather.7.cloned.1.call-update
  8.2 0.3 copy-done.2
  8.6 1.1 convert_multiply_fusion
  9.7 5.5 all-to-all-start.1
  15.2 0.5 convert_select_fusion
  15.7 2.0 select_multiply_fusion
  17.7 0.9 mul.48
  18.8 1.2 fusion.34
  22.7 0.9 select_n.75
  23.8 192.5 %sort.15 = (s32[4,65536]{1,0:T(4,128)}, f32[4,65536]{1,0:T(4,128)}) sort(s32[4,65536]{1,0:T(4,128)S(1)} %bitcast.33, f32[4,65536]{1,0:T(4,128)S(1)} %bitcast.34), dimensions={1}, to_apply=%region_0.1 | sort | flops 4718592 | bytes 4194304 | tf_op jit(solution)/shard_map/sort | solution.py:647
  216.3 0.6 pad.25.w_output.refs_3_
  216.9 0.5 iota_compare_fusion.3
  217.4 0.5 compare_select_fusion.1
  218.0 4.2 all-to-all-start
  222.2 2.1 convert_bitcast_fusion.w_ref
  224.3 11.5 all-to-all-done
  235.8 0.9 reshape.125
  236.7 0.7 copy.28
  237.4 0.5 copy.41
  237.9 1.0 copy-done
  238.9 1.1 broadcast_multiply_fusion.1.idx_hbm
  240.0 276.9 %layer_one.1 = (bf16[16384,256]{1,0:T(8,128)(2,1)}, bf16[16384,128]{1,0:T(8,128)(2,1)}) custom-call(s32[262144]{0:T(1024)} %broadcast_multiply_fusion.1.idx_hbm, f32[4,4,16384]{2,1,0:T(4,128)} %convert_bitcast_fusion.w_ref, bf16[131072,128]{1,0:T(8,128)(2,1)} %all-gather.7.cloned.1.call-done.x_hbm, bf16[128,256]{1,0:T(8,128)(2,1)} %w_hidden.1, ...), custom_call_target="tpu_custom_call" | custom-call | flops 199999995904 | bytes 100000000 | tf_op jit(solution)/shard_map/layer_one/pallas_call | solution.py:479
  516.9 2.6 fusion.32
  519.5 2.7 fusion.8
  522.5 2.1 convert_reduce_fusion
  524.6 2.4 reshape.128.col_ref
  527.1 0.7 reshape.130
  527.9 4.1 reshape.129.w_ref
  532.2 0.6 copy-done.10
  533.3 0.7 convert_reduce_fusion.1.over_ref
  534.0 0.5 fusion.28.active_ref
  534.5 0.6 fusion.25.base_ref
  535.1 1.0 broadcast_multiply_fusion.idx_hbm
  536.1 47.0 %all-gather.9.cloned.1.call-done.p_hbm = bf16[43776,128]{1,0:T(8,128)(2,1)} async-done(((bf16[5472,128]{1,0:T(8,128)(2,1)}), bf16[43776,128]{1,0:T(8,128)(2,1)}) %all-gather.9.cloned.1.call-update) | async-done | bytes 11206672 | tf_op jit(solution)/shard_map/all_gather | solution.py:656
  583.1 5.8 fusion.31
  589.0 0.8 copy-done.8
  589.8 0.5 scatter.9.node_ref
  590.3 0.8 slice.102
  591.2 0.7 add_reduce_fusion
  592.6 238.8 %layer_two.1 = (bf16[5472,128]{1,0:T(8,128)(2,1)}, f32[8,128]{1,0:T(8,128)}) custom-call(s32[262144]{0:T(1024)} %bitcast.30, f32[4,4,16384]{2,1,0:T(4,128)} %convert_bitcast_fusion.w_ref, bf16[43776,128]{1,0:T(8,128)(2,1)} %all-gather.9.cloned.1.call-done.p_hbm, f32[8,16384]{1,0:T(8,128)} %copy-done.5, f32[1]{0:T(128)} %bitcast.15.count_ref), custom_call_target="tpu_custom_call" | custom-call | flops 199999995904 | bytes 100000000 | tf_op jit(solution)/shard_map/layer_two/pallas_call | solution.py:500
  831.5 58.8 %all-gather.13.cloned.1.call-done.refs_0_ = bf16[21888,128]{1,0:T(8,128)(2,1)} async-done(((bf16[5472,128]{1,0:T(8,128)(2,1)}), bf16[21888,128]{1,0:T(8,128)(2,1)}) %all-gather.13.cloned.1.call-update) | async-done | bytes 5603344 | tf_op jit(solution)/shard_map/all_gather | solution.py:666
  890.6 227.3 %shard_map.103 = (f32[5472,128]{1,0:T(8,128)}, f32[5472,128]{1,0:T(8,128)}) custom-call(s32[4]{0:T(128)} %fusion.28.active_ref, s32[64]{0:T(128)} %convert_reduce_fusion.1.over_ref, s32[1024]{0:T(1024)} %fusion.25.base_ref, s32[1024]{0:T(1024)} %copy-done.10, s32[262144]{0:T(1024)} %bitcast.32, s32[16,1,16384]{2,1,0:T(1,128)} %reshape.128.col_ref, ...), custom_call_target="tpu_custom_call" | custom-call | flops 199999995904 | bytes 100000000 | tf_op jit(solution)/shard_map/pallas_call | solution.py:536
  1117.9 5.4 collective-permute-done
  1123.2 3.2 add_convert_fusion.2
  1126.5 71.6 %all-gather.17.cloned.1.call-done = bf16[43776,128]{1,0:T(8,128)(2,1)} async-done(((bf16[5472,128]{1,0:T(8,128)(2,1)}), bf16[43776,128]{1,0:T(8,128)(2,1)}) %all-gather.17.cloned.1.call-update) | async-done | bytes 11206672 | tf_op jit(solution)/shard_map/all_gather | solution.py:675
  1198.1 6.0 constant_dynamic-slice_fusion.1.refs_2_
  1204.1 265.0 %shard_map.104 = (f32[16384,256]{1,0:T(8,128)}, f32[16384,256]{1,0:T(8,128)}) custom-call(s32[4]{0:T(128)} %fusion.28.active_ref, s32[64]{0:T(128)} %convert_reduce_fusion.1.over_ref, s32[1024]{0:T(1024)} %fusion.25.base_ref, s32[1024]{0:T(1024)} %copy-done.10, s32[262144]{0:T(1024)} %broadcast_multiply_fusion.idx_hbm, s32[16,1,16384]{2,1,0:T(1,128)} %reshape.128.col_ref, ...), custom_call_target="tpu_custom_call" | custom-call | flops 199999995904 | bytes 100000000 | tf_op jit(solution)/shard_map/pallas_call | solution.py:536
  1469.1 0.3 collective-permute-start.1
  1469.4 0.6 reduce_sum.39
  1470.6 4.9 fusion.30
  1475.6 2.0 copy.32
  1477.6 1.7 copy.33
  1479.3 1.2 copy.34
  1480.5 3.2 concatenate.14
  1483.7 5.7 fusion.1
  1489.5 5.1 collective-permute-done.1
  1494.6 13.7 fusion
  1508.4 0.7 pad.29.x_ref
  1509.2 25.1 %all_reduce.1 = f32[576,128]{1,0:T(8,128)} custom-call(f32[576,128]{1,0:T(8,128)} %pad.29.x_ref), custom_call_target="tpu_custom_call" | custom-call | tf_op jit(solution)/shard_map/all_reduce/pallas_call | solution.py:612
  1534.3 1.2 slice.98
  1535.5 0.9 slice.99
  1536.4 0.9 slice.100
  1537.3 0.7 reshape.136
  1538.0 0.7 copy.36
  (55 shorter events, 2.5 us)
Async XLA Ops:
  7.2 1.0 copy-start.3
  7.2 1.4 copy-start.2
  7.2 232.8 %all-gather.7.cloned.1.call-start = ((), (), s32[]{:S(2)}) async-start(), calls=%async_computation.2 | async-start | bytes 37748736 | tf_op jit(solution)/shard_map/all_gather | solution.py:639
  9.7 208.3 %all-to-all-start.1 = ((bf16[4,4,16384]{2,0,1:T(4,128)(2,1)}), bf16[4,4,16384]{2,0,1:T(4,128)(2,1)}, u32[]{:S(2)}, u32[]{:S(2)}) async-start(bf16[4,4,16384]{2,0,1:T(4,128)(2,1)} %bitcast.7), calls=%async_computation.1 | async-start | bytes 1048576 | tf_op jit(solution)/shard_map/all_to_all | solution.py:642
  15.7 3.1 copy-start.7
  17.7 5.9 copy-start.9
  218.0 17.8 %all-to-all-start = ((s32[4,4,16384]{2,0,1:T(4,128)}), s32[4,4,16384]{2,0,1:T(4,128)S(1)}, u32[]{:S(2)}, u32[]{:S(2)}) async-start(s32[4,4,16384]{2,0,1:T(4,128)} %bitcast.4), calls=%async_computation | async-start | bytes 2097152 | tf_op jit(solution)/shard_map/all_to_all | solution.py:641
  222.2 360.9 %all-gather.9.cloned.1.call-start = ((), (), s32[]{:S(2)}) async-start(), calls=%async_computation.3 | async-start | bytes 12607488 | tf_op jit(solution)/shard_map/all_gather | solution.py:656
  237.9 1.0 copy-start
  516.9 2.6 copy-start.12
  516.9 2.6 copy-start.13
  519.5 3.0 copy-start.4
  522.3 309.2 %all-gather.11.cloned.1.call-start = ((), (), s32[]{:S(2)}) async-start(), calls=%async_computation.4 | async-start | bytes 20971520 | tf_op jit(solution)/shard_map/all_gather | solution.py:658
  527.9 8.2 copy-start.1
  532.2 0.6 copy-start.10
  588.9 0.8 copy-start.8
  588.9 0.9 copy-start.6
  588.9 301.4 %all-gather.13.cloned.1.call-start = ((), (), s32[]{:S(2)}) async-start(), calls=%async_computation.5 | async-start | bytes 7004160 | tf_op jit(solution)/shard_map/all_gather | solution.py:666
  590.3 2.3 copy-start.5
  831.5 295.0 %all-gather.15.cloned.1.call-start = ((), (), s32[]{:S(2)}) async-start(), calls=%async_computation.6 | async-start | bytes 20971520 | tf_op jit(solution)/shard_map/all_gather | solution.py:668
  890.3 307.8 %all-gather.17.cloned.1.call-start = ((), (), s32[]{:S(2)}) async-start(), calls=%async_computation.7 | async-start | bytes 12607488 | tf_op jit(solution)/shard_map/all_gather | solution.py:675
  1117.8 5.4 collective-permute-start
  1204.1 265.3 %copy-start.11 = (f32[8,128]{1,0:T(8,128)S(1)}, f32[8,128]{1,0:T(8,128)}, u32[]{:S(2)}) copy-start(f32[8,128]{1,0:T(8,128)} %get-tuple-element.84) | copy-start | bytes 12292
  1469.1 25.5 %collective-permute-start.1 = (f32[16384,256]{1,0:T(8,128)}, f32[16384,256]{1,0:T(8,128)}, u32[]{:S(2)}, u32[]{:S(2)}) collective-permute-start(f32[16384,256]{1,0:T(8,128)} %get-tuple-element.83), channel_id=1, source_target_pairs={{0,1},{1,0},{2,3},{3,2},{4,5},{5,4},{6,7},{7,6}} | collective-permute-start | bytes 50331656 | tf_op jit(solution)/shard_map/ppermute | solution.py:687
Sparse Core Ops, SparseCore 0:
  9.8 157.9 all-gather.6
  522.4 60.6 all-gather.8
  589.1 151.7 all-gather.10
  831.6 58.6 all-gather.12
  891.9 151.7 all-gather.14
  1126.6 71.4 all-gather.16

commit v5 on v4

--- a/solution.py
+++ b/solution.py
@@ -54,13 +54,13 @@
             table[pl.ds(width * first + part, rows, stride=width), :] = piece
 
 
-def stream_rows(source, buffer, sems, phase, phases, total, use):
+def stream_rows(source, buffer, sems, phase, phases, total, use, shift=0):
     slots, chunk = buffer.shape[0], buffer.shape[1]
     steps = total // chunk
     assert steps % slots == 0
 
     def copy(step, slot):
-        start = pl.multiple_of(phase * total + step * chunk, 16)
+        start = pl.multiple_of(shift + phase * total + step * chunk, 16)
         return pltpu.make_async_copy(source.at[pl.ds(start, chunk), :], buffer.at[slot], sems.at[slot])
 
     @pl.when(phase == 0)
@@ -190,7 +190,7 @@
         finish_rows(acc, use)
 
 
-def unpack_table(table, p_hbm, p_buf, sems, phase, phases, blocks, nodes):
+def unpack_table(table, p_hbm, p_buf, sems, phase, phases, blocks, nodes, first_block=0):
     packed = packed_rows(nodes)
     piece = packed // 18
 
@@ -208,7 +208,7 @@
 
         lax.fori_loop(0, 18, body, 0)
 
-    stream_rows(p_hbm, p_buf, sems, phase, phases, blocks * packed, use)
+    stream_rows(p_hbm, p_buf, sems, phase, phases, blocks * packed, use, first_block * packed)
 
 
 def pack_lanes():
@@ -298,6 +298,7 @@
         packed_sums, refs = refs[0], refs[1:]
     buffers, sems = refs[0::2], refs[1::2]
     stages = [stage_a, stage_b]
+    phases = active_ref.shape[0] - 1
     phase, tile = pl.program_id(0), pl.program_id(1)
     steps = pl.num_programs(1) * INNER
     total = pl.num_programs(0) * steps
@@ -315,7 +316,7 @@
 
     @pl.when(tile == 0)
     def _():
-        build(sources, buffers, sems, phase, pl.num_programs(0), table)
+        build(sources, buffers, sems, phase, pl.num_programs(0), active_ref[phases], table)
 
     def gathered(stage):
         lanes = []
@@ -430,15 +431,15 @@
             copy.wait()
 
 
-def build_packed(nodes, sources, buffers, sems, phase, phases, table):
+def build_packed(nodes, sources, buffers, sems, phase, phases, first_block, table):
     unpack_table(table, sources[0], buffers[0], sems[0], phase, phases, 1, nodes)
 
 
-def build_dz(nodes, sources, buffers, sems, phase, phases, table):
+def build_dz(nodes, sources, buffers, sems, phase, phases, first_block, table):
     z_first, z_second, b_hbm, w_out = sources
     z_buf, b_buf, back = buffers
     half = nodes // 2
-    unpack_table(back, b_hbm, b_buf, sems[1], phase, phases, 1, nodes)
+    unpack_table(back, b_hbm, b_buf, sems[1], phase, phases, 1, nodes, first_block)
 
     def use(buf, offset):
         for sub in range(0, z_buf.shape[2], 256):
@@ -514,7 +515,7 @@
 
 def segment_product(build, plan, sources, specs, buffers, num_out, width, rows):
     ids_by_width, cols, weights, scalars = plan
-    phases = scalars[0].shape[0]
+    phases = scalars[0].shape[0] - 1
     steps, per_step = cols.shape[0] // phases, cols.shape[2]
     any_spec = pl.BlockSpec(memory_space=pl.ANY)
     tile_spec = pl.BlockSpec((1, 1, per_step), lambda p, t, *_: (p * steps + t, 0, 0))
@@ -553,7 +554,7 @@
     return keys, weights.transpose(1, 0, 2).reshape(col_blocks, slots * blk_nodes)
 
 
-def make_plan(keys, weights, blk_nodes):
+def make_plan(keys, weights, blk_nodes, first_block):
     col_nodes = 2 * blk_nodes
     cols, rows = keys // blk_nodes, keys % blk_nodes
     chunked = cols.reshape(-1, CHUNK)
@@ -562,6 +563,7 @@
     over = jnp.max((last >= base + WINDOW).astype(jnp.int32).reshape(-1, STEP_CHUNKS), axis=1)
     count = jnp.sum((cols < col_nodes).astype(jnp.int32), axis=1)
     active = jnp.maximum((count + STEP_CHUNKS * CHUNK - 1) // (STEP_CHUNKS * CHUNK), 1)
+    active = jnp.concatenate([active, first_block.reshape(1)])
     tiles = (-1, 1, INNER * STEP_CHUNKS * CHUNK)
     ids_by_width = (rows.reshape(-1), 2 * rows.reshape(-1))
     return ids_by_width, cols.reshape(tiles), weights.reshape(tiles), (active, over, base, last)
@@ -646,7 +648,7 @@
         keys, edge_w = edge_lists(cols_blk, mask_blk, vals_blk, col_size, blk_nodes, (1 - row_i) * blk_nodes)
         edges = lax.sort((keys, edge_w), dimension=1, num_keys=1, is_stable=False)
         x_all, edges = lax.optimization_barrier((x_all, edges))
-        plan = make_plan(*edges, blk_nodes)
+        plan = make_plan(*edges, blk_nodes, row_i * col_size)
 
         z_one, proj_two = layer_one(own_cols * 2, own_w, x_all, w_hidden, w_out_pad)
         count = jnp.sum(train_blk)
@@ -654,7 +656,8 @@
         lane_ids = lax.broadcasted_iota(jnp.int32, (packed, LANES), 1)
         counts = jnp.where(lane_ids == spare, count // 128, jnp.where(lane_ids == spare + 1, count % 128, 0))
         p_all = lax.all_gather(pack_nodes(proj_two[:, :classes]) + counts.astype(jnp.bfloat16), both_axes, axis=0, tiled=True)
-        z_one, p_all, plan = lax.optimization_barrier((z_one, p_all, plan))
+        feat_src = lax.dynamic_slice_in_dim(x_all, (col_j * row_size + row_i) * blk_nodes, blk_nodes, 0)
+        z_one, p_all, plan, feat_src = lax.optimization_barrier((z_one, p_all, plan, feat_src))
         z_first = lax.all_gather(z_one[:blk_nodes // 2], "col", axis=0, tiled=True)
         counts = p_all.reshape(row_size * col_size, packed, LANES)[:, 0, spare:spare + 2].astype(jnp.float32)
         train_count = jnp.maximum(jnp.sum(counts[:, 0] * 128.0 + counts[:, 1]), 1.0)
@@ -673,19 +676,17 @@
         back_two = (keep_two + lax.ppermute(send_two, "row", swap)).astype(jnp.bfloat16)
         z_second, back_two = lax.optimization_barrier((z_second, back_two))
         back_all = lax.all_gather(back_two, ("col", "row"), axis=0, tiled=True)
-        back_rows = lax.dynamic_slice_in_dim(back_all, row_i * col_size * packed, col_size * packed, 0)
-        back_own = lax.dynamic_slice_in_dim(back_rows, col_j * packed, packed, 0)
+        back_own = lax.dynamic_slice_in_dim(back_all, (row_i * col_size + col_j) * packed, packed, 0)
         back_own = jnp.concatenate([back_own[:, q * pack_lanes():q * pack_lanes() + classes] for q in range(PACK)], axis=0)[:blk_nodes]
         h_one = jnp.maximum(z_one, 0)
         grad_w_output = lax.dot_general(h_one, back_own, CONTRACT_ROWS, preferred_element_type=jnp.float32)
 
         send_one, keep_one = segment_product(
-            build_dz, plan, [z_first, z_second, back_rows, w_out_pad], [any_spec, any_spec, any_spec, whole],
+            build_dz, plan, [z_first, z_second, back_all, w_out_pad], [any_spec, any_spec, any_spec, whole],
             [pltpu.VMEM((2, 4, 1024, 2 * LANES), jnp.bfloat16), pltpu.SemaphoreType.DMA((2, 4)), *row_bufs,
              pltpu.VMEM((blk_nodes + 128, LANES), jnp.bfloat16)],
             col_nodes, 2, blk_nodes)
         back_one = (keep_one + lax.ppermute(send_one, "row", swap)).astype(jnp.bfloat16)
-        feat_src = lax.dynamic_slice_in_dim(x_all, (col_j * row_size + row_i) * blk_nodes, blk_nodes, 0)
         grad_w_hidden = lax.dot_general(feat_src, back_one, CONTRACT_ROWS, preferred_element_type=jnp.float32)
         feat, hid = w_hidden.shape
         out_pad = jnp.pad(grad_w_output, ((0, 0), (0, LANES - classes)))

time: 1560 us -> 1550 us (level)
  no operation moved by 1% of the time
where the time goes in v5:
time: 1550 us; the launch traced here: 1540 us
  Pallas kernels  1030 us (66%)
  other arithmetic  214 us (14%)
  waiting for transfers between devices  196 us (13%)
  local copies, waits for them, and re-layouts  47.1 us (3%)
  between operations  18.8 us (1%)
  matrix products  18.6 us (1%)
    pallas_call x2, Pallas kernels, segment_product(): pl.pallas_call(functools.partial(segment_kernel, width, rows, len(sources...  492 us
    pallas_call x1, Pallas kernels, layer_one(): pl.pallas_call(layer_one_kernel, grid=(phases, rows // (INNER * STEP_SUBS...  277 us
    pallas_call x1, Pallas kernels, layer_two(): pl.pallas_call(functools.partial(layer_two_kernel, rows, classes), grid=(...  239 us
    sort x1, other arithmetic, device_step(): edges = lax.sort((keys, edge_w), dimension=1, num_keys=1, is_stable=False)  193 us
    all_gather x1, waiting for transfers between devices, device_step(): back_all = lax.all_gather(back_two, ('col', 'row'), axis=0, tiled=True)  71.6 us
    all_gather x1, waiting for transfers between devices, device_step(): grad_rows = lax.all_gather(grad_two, 'col', axis=0, tiled=True)  58.8 us
    all_gather x1, waiting for transfers between devices, device_step(): lax.all_gather(pack_nodes(proj_two[:, :classes]) + counts.astype(jnp.bflo...  43.1 us
  transfers between devices with their start and end apart: 10, of which 6 were waited for; matrix products, arithmetic and copies ran while one was open for 16% of the time, Pallas kernels for 30%

profile of v5, /device:TPU:0, one launch (start us, length us, event | category | flops | bytes accessed | tf_op | source)
XLA Modules:
  0.0 1538.9 jit_solution(4580487033535854623)
XLA Ops:
  7.2 0.7 all-gather.7.cloned.1.call-update
  8.2 0.3 copy-done.3
  8.6 1.1 convert_multiply_fusion
  9.6 5.5 all-to-all-start.1
  15.2 0.5 convert_select_fusion
  15.7 2.0 select_multiply_fusion
  17.7 0.9 mul.50
  18.8 1.3 fusion.32
  22.7 0.9 select_n.68
  23.7 192.7 %sort.15 = (s32[4,65536]{1,0:T(4,128)}, f32[4,65536]{1,0:T(4,128)}) sort(s32[4,65536]{1,0:T(4,128)S(1)} %bitcast.35, f32[4,65536]{1,0:T(4,128)S(1)} %bitcast.36), dimensions={1}, to_apply=%region_0.1 | sort | flops 4718592 | bytes 4194304 | tf_op jit(solution)/shard_map/sort | solution.py:649
  216.4 0.6 pad.25.w_output.refs_3_
  217.1 0.5 iota_compare_fusion.3
  217.6 0.5 compare_select_fusion.1
  218.1 4.2 all-to-all-start
  222.3 2.1 convert_bitcast_fusion.w_ref
  224.4 11.5 all-to-all-done
  236.0 0.9 reshape.126
  236.8 0.7 copy.28
  237.5 0.5 copy.41
  238.1 1.0 copy-done.1
  239.0 1.1 broadcast_multiply_fusion.1.idx_hbm
  240.1 276.9 %layer_one.1 = (bf16[16384,256]{1,0:T(8,128)(2,1)}, bf16[16384,128]{1,0:T(8,128)(2,1)}) custom-call(s32[262144]{0:T(1024)} %broadcast_multiply_fusion.1.idx_hbm, f32[4,4,16384]{2,1,0:T(4,128)} %convert_bitcast_fusion.w_ref, bf16[131072,128]{1,0:T(8,128)(2,1)} %all-gather.7.cloned.1.call-done.x_hbm, bf16[128,256]{1,0:T(8,128)(2,1)} %w_hidden.1, ...), custom_call_target="tpu_custom_call" | custom-call | flops 199999995904 | bytes 100000000 | tf_op jit(solution)/shard_map/layer_one/pallas_call | solution.py:480
  517.1 2.6 fusion.30
  519.7 2.7 fusion.7
  522.7 2.1 convert_reduce_fusion
  524.8 2.4 reshape.131.col_ref
  527.3 0.7 reshape.134
  528.1 4.1 reshape.132.w_ref
  532.4 0.6 copy-done.11
  533.6 0.6 pad_add_fusion.active_ref
  534.1 0.7 convert_reduce_fusion.1.over_ref
  534.8 0.6 fusion.24.base_ref
  535.4 3.7 constant_dynamic-slice_fusion.1
  539.1 1.1 broadcast_multiply_fusion.idx_hbm
  540.2 43.1 %all-gather.9.cloned.1.call-done.p_hbm = bf16[43776,128]{1,0:T(8,128)(2,1)} async-done(((bf16[5472,128]{1,0:T(8,128)(2,1)}), bf16[43776,128]{1,0:T(8,128)(2,1)}) %all-gather.9.cloned.1.call-update) | async-done | bytes 11206672 | tf_op jit(solution)/shard_map/all_gather | solution.py:658
  583.2 5.7 fusion.29
  589.1 0.8 copy-done.9
  589.9 0.5 scatter.9.node_ref
  590.4 0.8 slice.102
  591.3 0.6 add_reduce_fusion
  592.5 238.8 %layer_two.1 = (bf16[5472,128]{1,0:T(8,128)(2,1)}, f32[8,128]{1,0:T(8,128)}) custom-call(s32[262144]{0:T(1024)} %bitcast.32, f32[4,4,16384]{2,1,0:T(4,128)} %convert_bitcast_fusion.w_ref, bf16[43776,128]{1,0:T(8,128)(2,1)} %all-gather.9.cloned.1.call-done.p_hbm, f32[8,16384]{1,0:T(8,128)} %copy-done.6, f32[1]{0:T(128)} %bitcast.16.count_ref), custom_call_target="tpu_custom_call" | custom-call | flops 199999995904 | bytes 100000000 | tf_op jit(solution)/shard_map/layer_two/pallas_call | solution.py:501
  831.4 58.8 %all-gather.13.cloned.1.call-done.refs_0_ = bf16[21888,128]{1,0:T(8,128)(2,1)} async-done(((bf16[5472,128]{1,0:T(8,128)(2,1)}), bf16[21888,128]{1,0:T(8,128)(2,1)}) %all-gather.13.cloned.1.call-update) | async-done | bytes 5603344 | tf_op jit(solution)/shard_map/all_gather | solution.py:669
  890.5 227.2 %shard_map.103 = (f32[5472,128]{1,0:T(8,128)}, f32[5472,128]{1,0:T(8,128)}) custom-call(s32[5]{0:T(128)} %pad_add_fusion.active_ref, s32[64]{0:T(128)} %convert_reduce_fusion.1.over_ref, s32[1024]{0:T(1024)} %fusion.24.base_ref, s32[1024]{0:T(1024)} %copy-done.11, s32[262144]{0:T(1024)} %bitcast.34, s32[16,1,16384]{2,1,0:T(1,128)} %reshape.131.col_ref, ...), custom_call_target="tpu_custom_call" | custom-call | flops 199999995904 | bytes 100000000 | tf_op jit(solution)/shard_map/pallas_call | solution.py:537
  1117.7 5.4 collective-permute-done
  1123.1 3.2 add_convert_fusion.2
  1126.3 71.6 %all-gather.17.cloned.1.call-done.refs_2_ = bf16[43776,128]{1,0:T(8,128)(2,1)} async-done(((bf16[5472,128]{1,0:T(8,128)(2,1)}), bf16[43776,128]{1,0:T(8,128)(2,1)}) %all-gather.17.cloned.1.call-update) | async-done | bytes 11206672 | tf_op jit(solution)/shard_map/all_gather | solution.py:678
  1197.9 264.9 %shard_map.104 = (f32[16384,256]{1,0:T(8,128)}, f32[16384,256]{1,0:T(8,128)}) custom-call(s32[5]{0:T(128)} %pad_add_fusion.active_ref, s32[64]{0:T(128)} %convert_reduce_fusion.1.over_ref, s32[1024]{0:T(1024)} %fusion.24.base_ref, s32[1024]{0:T(1024)} %copy-done.11, s32[262144]{0:T(1024)} %broadcast_multiply_fusion.idx_hbm, ...), custom_call_target="tpu_custom_call" | custom-call | flops 199999995904 | bytes 100000000 | tf_op jit(solution)/shard_map/pallas_call | solution.py:537
  1462.8 0.3 collective-permute-start.1
  1463.1 0.6 reduce_sum.39
  1464.4 4.8 fusion.28
  1469.2 1.8 copy.32
  1471.0 1.8 copy.33
  1472.7 1.4 copy.34
  1474.2 3.2 concatenate.18
  1477.4 5.9 fusion.1
  1483.3 5.0 collective-permute-done.1
  1488.3 12.7 fusion
  1501.2 0.7 pad.29.x_ref
  1501.9 25.2 %all_reduce.1 = f32[576,128]{1,0:T(8,128)} custom-call(f32[576,128]{1,0:T(8,128)} %pad.29.x_ref), custom_call_target="tpu_custom_call" | custom-call | tf_op jit(solution)/shard_map/all_reduce/pallas_call | solution.py:614
  1527.2 1.2 slice.98
  1528.4 0.9 slice.99
  1529.3 0.9 slice.100
  1530.2 0.7 reshape.140
  1530.9 0.7 copy.36
  (58 shorter events, 2.5 us)
Async XLA Ops:
  7.2 1.0 copy-start.4
  7.2 1.4 copy-start.3
  7.2 232.9 %all-gather.7.cloned.1.call-start = ((), (), s32[]{:S(2)}) async-start(), calls=%async_computation.2 | async-start | bytes 37748736 | tf_op jit(solution)/shard_map/all_gather | solution.py:641
  9.6 208.5 %all-to-all-start.1 = ((bf16[4,4,16384]{2,0,1:T(4,128)(2,1)}), bf16[4,4,16384]{2,0,1:T(4,128)(2,1)}, u32[]{:S(2)}, u32[]{:S(2)}) async-start(bf16[4,4,16384]{2,0,1:T(4,128)(2,1)} %bitcast.3), calls=%async_computation.1 | async-start | bytes 1048576 | tf_op jit(solution)/shard_map/all_to_all | solution.py:644
  15.7 3.1 copy-start.8
  17.7 5.9 copy-start.10
  218.1 17.8 %all-to-all-start = ((s32[4,4,16384]{2,0,1:T(4,128)}), s32[4,4,16384]{2,0,1:T(4,128)S(1)}, u32[]{:S(2)}, u32[]{:S(2)}) async-start(s32[4,4,16384]{2,0,1:T(4,128)} %bitcast), calls=%async_computation | async-start | bytes 2097152 | tf_op jit(solution)/shard_map/all_to_all | solution.py:643
  222.3 360.9 %all-gather.9.cloned.1.call-start = ((), (), s32[]{:S(2)}) async-start(), calls=%async_computation.3 | async-start | bytes 12607488 | tf_op jit(solution)/shard_map/all_gather | solution.py:658
  238.1 1.0 copy-start.1
  517.0 2.6 copy-start.13
  517.1 2.6 copy-start.14
  519.7 3.0 copy-start.5
  522.4 308.9 %all-gather.11.cloned.1.call-start = ((), (), s32[]{:S(2)}) async-start(), calls=%async_computation.4 | async-start | bytes 20971520 | tf_op jit(solution)/shard_map/all_gather | solution.py:661
  528.1 11.1 copy-start.2
  532.4 0.6 copy-start.11
  589.0 0.8 copy-start.9
  589.0 0.9 copy-start.7
  589.0 301.2 %all-gather.13.cloned.1.call-start = ((), (), s32[]{:S(2)}) async-start(), calls=%async_computation.5 | async-start | bytes 7004160 | tf_op jit(solution)/shard_map/all_gather | solution.py:669
  590.4 2.1 copy-start.6
  831.4 294.9 %all-gather.15.cloned.1.call-start = ((), (), s32[]{:S(2)}) async-start(), calls=%async_computation.6 | async-start | bytes 20971520 | tf_op jit(solution)/shard_map/all_gather | solution.py:671
  890.2 307.7 %all-gather.17.cloned.1.call-start = ((), (), s32[]{:S(2)}) async-start(), calls=%async_computation.7 | async-start | bytes 12607488 | tf_op jit(solution)/shard_map/all_gather | solution.py:678
  1117.7 5.4 collective-permute-start
  1197.9 265.2 %copy-start.12 = (f32[8,128]{1,0:T(8,128)S(1)}, f32[8,128]{1,0:T(8,128)}, u32[]{:S(2)}) copy-start(f32[8,128]{1,0:T(8,128)} %get-tuple-element.86) | copy-start | bytes 12292
  1462.8 25.5 %collective-permute-start.1 = (f32[16384,256]{1,0:T(8,128)}, f32[16384,256]{1,0:T(8,128)}, u32[]{:S(2)}, u32[]{:S(2)}) collective-permute-start(f32[16384,256]{1,0:T(8,128)} %get-tuple-element.85), channel_id=1, source_target_pairs={{0,1},{1,0},{2,3},{3,2},{4,5},{5,4},{6,7},{7,6}} | collective-permute-start | bytes 50331656 | tf_op jit(solution)/shard_map/ppermute | solution.py:689
  1477.4 10.9 copy-start
Sparse Core Ops, SparseCore 0:
  9.8 157.9 all-gather.6
  522.6 60.6 all-gather.8
  589.1 151.7 all-gather.10
  831.5 58.6 all-gather.12
  891.8 151.7 all-gather.14
  1126.4 71.4 all-gather.16
